TPU v7x, 8 devices: a whole 2x2x1 slice. The times are simulated.
8 devices in a mesh: dp: 2 (over z, y), tp: 4 (over x, core).
Axes of the slice: x: 2, y: 2, z: 1, core: 2. Of those that a mesh axis runs over, the one named last changes fastest.
Arguments:
- hidden: bfloat16 [4, 512, 3072], P('dp'), parts along dimension 0
- lengths: int32 [4], P('dp'), parts along dimension 0
- w_query: bfloat16 [2, 3072, 16, 256], P(None, None, 'tp')
- w_key: bfloat16 [2, 3072, 16, 256], P(None, None, 'tp')
- w_value: bfloat16 [2, 3072, 16, 256], P(None, None, 'tp')
- w_out: bfloat16 [2, 16, 256, 3072], P(None, 'tp')
- w_gate: bfloat16 [2, 3072, 24576], P(None, None, 'tp')
- w_up: bfloat16 [2, 3072, 24576], P(None, None, 'tp')
- w_down: bfloat16 [2, 24576, 3072], P(None, 'tp')
- norm_attn: float32 [2, 3072], replicated
- norm_mlp: float32 [2, 3072], replicated
Outputs:
- output 1: bfloat16 [4, 512, 3072], P('dp'), parts along dimension 0
- output 2: bfloat16 [2, 4, 16, 512, 256], P(None, 'dp', 'tp'), parts along dimension 1
- output 3: bfloat16 [2, 4, 16, 512, 256], P(None, 'dp', 'tp'), parts along dimension 1
There are 2 independent parts. A program takes and returns all parts, laid end to end along the dimension named above; an argument that names none is the same for every part.
All inputs are finite; a program needn't handle non-finite values.
Results may differ from a plain program's by a relative error of at most 0.0179353.
Values are sent between devices in bfloat16 or wider.
A program may use at most 1.25 GiB of HBM per device.

v0:
```python
import jax
import jax.numpy as jnp
from jax import lax
from jax.sharding import PartitionSpec as P

RMS_EPS = 1e-6
ROPE_BASE = 10000.0


def rms_norm(x_in, norm_gain):
    x_f32 = x_in.astype(jnp.float32)
    mean_sq = jnp.mean(x_f32 * x_f32, axis=-1, keepdims=True)
    return (x_f32 * lax.rsqrt(mean_sq + RMS_EPS) * (1.0 + norm_gain)).astype(jnp.bfloat16)


def rope_tables(seq_len, head_dim):
    half_dim = head_dim // 2
    inv_freq = ROPE_BASE ** (-jnp.arange(half_dim, dtype=jnp.float32) * (2.0 / head_dim))
    angles = jnp.arange(seq_len, dtype=jnp.float32)[:, None] * inv_freq[None, :]
    return jnp.cos(angles)[:, None, :], jnp.sin(angles)[:, None, :]


def apply_rope(x_in, cos_t, sin_t):
    half_dim = x_in.shape[-1] // 2
    x_low = x_in[..., :half_dim]
    x_high = x_in[..., half_dim:]
    return jnp.concatenate([x_low * cos_t - x_high * sin_t, x_high * cos_t + x_low * sin_t], axis=-1)


def attention(normed, lengths, w_query, w_key, w_value, cos_t, sin_t):
    head_dim = w_query.shape[-1]
    seq_len = normed.shape[1]
    query = jnp.einsum("duo,ojf->dujf", normed, w_query, preferred_element_type=jnp.float32)
    keys = jnp.einsum("duo,ojf->dujf", normed, w_key, preferred_element_type=jnp.float32)
    values = jnp.einsum("duo,ojf->dujf", normed, w_value, preferred_element_type=jnp.float32).astype(jnp.bfloat16)
    query_rot = (apply_rope(query, cos_t, sin_t) * (head_dim ** -0.5)).astype(jnp.bfloat16)
    key_rot = apply_rope(keys, cos_t, sin_t).astype(jnp.bfloat16)
    scores = jnp.einsum("bqhd,bkhd->bhqk", query_rot, key_rot, preferred_element_type=jnp.float32)
    positions = jnp.arange(seq_len)
    allowed = (positions[None, None, :] <= positions[None, :, None]) & (positions[None, None, :] < lengths[:, None, None])
    scores = jnp.where(allowed[:, None, :, :], scores, -1e30)
    attn_probs = jax.nn.softmax(scores, axis=-1).astype(jnp.bfloat16)
    attn_out = jnp.einsum("bhqk,bkhd->bqhd", attn_probs, values, preferred_element_type=jnp.float32).astype(jnp.bfloat16)
    return attn_out, key_rot, values


def mlp_partial(normed, w_gate, w_up, w_down):
    gate_pre = jnp.einsum("bsm,mf->bsf", normed, w_gate, preferred_element_type=jnp.float32)
    up_proj = jnp.einsum("bsm,mf->bsf", normed, w_up, preferred_element_type=jnp.float32)
    hidden_act = (jax.nn.gelu(gate_pre, approximate=True) * up_proj).astype(jnp.bfloat16)
    return jnp.einsum("bsf,fm->bsm", hidden_act, w_down, preferred_element_type=jnp.float32)


def solution(mesh):
    head_cols = P(None, None, "tp", None)
    head_rows = P(None, "tp", None, None)
    ff_cols = P(None, None, "tp")
    ff_rows = P(None, "tp", None)

    def shard_body(hidden, lengths, w_query, w_key, w_value, w_out, w_gate, w_up, w_down, norm_attn, norm_mlp):
        cos_t, sin_t = rope_tables(hidden.shape[1], w_query.shape[-1])
        hidden_state = hidden
        key_list = []
        value_list = []
        for layer_idx in range(w_query.shape[0]):
            normed = rms_norm(hidden_state, norm_attn[layer_idx])
            attn_out, key_rot, values = attention(normed, lengths, w_query[layer_idx], w_key[layer_idx], w_value[layer_idx], cos_t, sin_t)
            part_sum = jnp.einsum("bqhd,hdm->bqm", attn_out, w_out[layer_idx], preferred_element_type=jnp.float32).astype(jnp.bfloat16)
            summed = lax.psum(part_sum, "tp")
            hidden_state = (hidden_state.astype(jnp.float32) + summed.astype(jnp.float32)).astype(jnp.bfloat16)
            normed = rms_norm(hidden_state, norm_mlp[layer_idx])
            part_sum = mlp_partial(normed, w_gate[layer_idx], w_up[layer_idx], w_down[layer_idx]).astype(jnp.bfloat16)
            summed = lax.psum(part_sum, "tp")
            hidden_state = (hidden_state.astype(jnp.float32) + summed.astype(jnp.float32)).astype(jnp.bfloat16)
            key_list.append(jnp.swapaxes(key_rot, 1, 2))
            value_list.append(jnp.swapaxes(values, 1, 2))
        return hidden_state, jnp.stack(key_list), jnp.stack(value_list)

    return jax.shard_map(
        shard_body,
        mesh=mesh,
        in_specs=(P("dp"), P("dp"), head_cols, head_cols, head_cols, head_rows, ff_cols, ff_cols, ff_rows, P(), P()),
        out_specs=(P("dp"), P(None, "dp", "tp"), P(None, "dp", "tp")),
        check_vma=False,
    )
```

profile of v0, /device:TPU:0, one launch (start us, length us, event | category | flops | bytes accessed | tf_op | source)
XLA Modules:
  0.0 968.5 jit_solution(17726586729097892613)
XLA Ops:
  13.8 12.2 %fusion.150 = (bf16[1,3072,4,256]{3,2,1,0:T(4,128)(2,1)}, bf16[1,3072,4,256]{3,2,1,0:T(4,128)(2,1)}) fusion(bf16[2,3072,4,256]{3,2,1,0:T(4,128)(2,1)} %param.13), kind=kLoop, calls=%fused_computation.164 | loop fusion | bytes 25165824 | tf_op jit(solution)/shard_map/slice | solution.py:67
  26.0 10.7 %copy.34 = bf16[1,3072,4,256]{1,3,2,0:T(8,128)(2,1)} copy(bf16[1,3072,4,256]{3,2,1,0:T(4,128)(2,1)} %get-tuple-element.15) | data formatting | bytes 12582912
  36.6 11.9 %fusion.149 = (bf16[1,3072,4,256]{3,2,1,0:T(4,128)(2,1)}, bf16[1,3072,4,256]{3,2,1,0:T(4,128)(2,1)}) fusion(bf16[2,3072,4,256]{3,2,1,0:T(4,128)(2,1)} %param.14), kind=kLoop, calls=%fused_computation.163 | loop fusion | bytes 25165824 | tf_op jit(solution)/shard_map/slice | solution.py:67
  48.5 10.7 %copy.35 = bf16[1,3072,4,256]{1,3,2,0:T(8,128)(2,1)} copy(bf16[1,3072,4,256]{3,2,1,0:T(4,128)(2,1)} %get-tuple-element.13) | data formatting | bytes 12582912
  59.2 11.0 %fusion.76 = f32[2,512,4,256]{1,3,2,0:T(8,128)S(1)} fusion(bf16[1,3072,4,256]{1,3,2,0:T(8,128)(2,1)} %copy.34, bf16[2,512,3072]{2,1,0:T(8,128)(2,1)} %param.11, f32[3072]{0:T(1024)S(1)} %bitcast.151, f32[2,512]{1,0:T(2,128)S(1)} %add_rsqrt_fusion.3), kind=kOutput, calls=%fused_computation.92 | convolution fusion | flops 6455033856 | bytes 16793600 | tf_op jit(solution)/shard_map/duo,ojf->dujf/dot_general | solution.py:33
  70.3 8.4 fusion.74
  78.7 5.8 fusion.151
  84.6 8.5 fusion.118
  100.0 5.4 fusion.152
  105.4 13.9 %bitcast_convert_fusion.1 = bf16[2,512,3072]{2,1,0:T(8,128)(2,1)} fusion(bf16[2,4,256,3072]{3,2,1,0:T(8,128)(2,1)} %param.16, bf16[2,512,4,256]{3,1,2,0:T(8,128)(2,1)S(1)} %copy-done.18, f32[2,4,512,512]{2,3,1,0:T(8,128)} %get-tuple-element.37, f32[2,4,512]{2,1,0:T(4,128)S(1)} %get-tuple-element.36), kind=kOutput, calls=%fused_computation.69 | convolution fusion | flops 7524581376 | bytes 23085056 | tf_op jit(solution)/shard_map/bqhd,hdm->bqm/dot_general | solution.py:68
  120.7 115.5 %all-reduce.5.cloned.1.call-done = bf16[2,512,3072]{2,1,0:T(8,128)(2,1)} async-done(((bf16[2,512,3072]{2,1,0:T(8,128)(2,1)}), bf16[2,512,3072]{2,1,0:T(8,128)(2,1)}) %all-reduce.5.cloned.1.call-update) | async-done | bytes 6291472 | tf_op jit(solution)/shard_map/psum | solution.py:69
  236.1 10.2 %fusion.46 = (f32[2,512]{1,0:T(2,128)S(1)}, bf16[2,512,3072]{2,1,0:T(8,128)(2,1)}) fusion(bf16[2,512,3072]{2,1,0:T(8,128)(2,1)} %all-reduce.5.cloned.1.call-done, bf16[2,512,3072]{2,1,0:T(8,128)(2,1)} %param.11), kind=kLoop, calls=%fused_computation.56 | loop fusion | flops 22019072 | bytes 18878464 | tf_op jit(solution)/shard_map/reduce_sum | solution.py:12
  246.3 48.7 %fusion.12 = f32[2,512,6144]{2,1,0:T(8,128)} fusion(bf16[2,3072,6144]{2,1,0:T(8,128)(2,1)} %param.17, bf16[2,512,3072]{2,1,0:T(8,128)(2,1)} %get-tuple-element.11, f32[3072]{0:T(1024)S(1)} %bitcast.154, f32[2,512]{1,0:T(2,128)S(1)} %add_rsqrt_fusion.2), kind=kOutput, calls=%fused_computation.14 | convolution fusion | flops 38667288576 | bytes 69222400 | tf_op jit(solution)/shard_map/bsm,mf->bsf/dot_general | solution.py:48
  295.0 50.1 %fusion.28.clone.7 = bf16[2,512,6144]{2,1,0:T(8,128)(2,1)} fusion(f32[2,512,6144]{2,1,0:T(8,128)} %fusion.12, bf16[2,3072,6144]{2,1,0:T(8,128)(2,1)} %param.18, bf16[2,512,3072]{2,1,0:T(8,128)(2,1)S(1)} %copy-done.1, f32[3072]{0:T(1024)S(1)} %bitcast.155, f32[2,512]{1,0:T(2,128)S(1)} %add_rsqrt_fusion.2), kind=kOutput, calls=%fused_computation.30.clone.clone.clone.clone.clone.2 | convolution fusion | flops 38730203136 | bytes 81805312 | tf_op jit(solution)/shard_map/bsm,mf->bsf/dot_general | solution.py:49
  345.1 47.6 %fusion.84 = bf16[2,512,3072]{2,1,0:T(8,128)(2,1)} fusion(bf16[2,6144,3072]{2,1,0:T(8,128)(2,1)} %param.19, bf16[2,512,6144]{2,1,0:T(8,128)(2,1)} %fusion.28.clone.7), kind=kOutput, calls=%fused_computation.96 | convolution fusion | flops 38657851392 | bytes 56623104 | tf_op jit(solution)/shard_map/bsf,fm->bsm/dot_general | solution.py:51
  392.8 10.7 %copy.37 = bf16[1,3072,4,256]{1,3,2,0:T(8,128)(2,1)} copy(bf16[1,3072,4,256]{3,2,1,0:T(4,128)(2,1)} %get-tuple-element.14) | data formatting | bytes 12582912
  403.4 10.6 %copy.38 = bf16[1,3072,4,256]{1,3,2,0:T(8,128)(2,1)} copy(bf16[1,3072,4,256]{3,2,1,0:T(4,128)(2,1)} %get-tuple-element.12) | data formatting | bytes 12582912
  414.0 92.9 %all-reduce.7.cloned.1.call-done = bf16[2,512,3072]{2,1,0:T(8,128)(2,1)} async-done(((bf16[2,512,3072]{2,1,0:T(8,128)(2,1)}), bf16[2,512,3072]{2,1,0:T(8,128)(2,1)}) %all-reduce.7.cloned.1.call-update) | async-done | bytes 6291472 | tf_op jit(solution)/shard_map/psum | solution.py:73
  506.9 10.4 %fusion.50 = (f32[2,512]{1,0:T(2,128)S(1)}, bf16[2,512,3072]{2,1,0:T(8,128)(2,1)}) fusion(bf16[2,512,3072]{2,1,0:T(8,128)(2,1)} %all-reduce.7.cloned.1.call-done, bf16[2,512,3072]{2,1,0:T(8,128)(2,1)} %get-tuple-element.11), kind=kLoop, calls=%fused_computation.60 | loop fusion | flops 22019072 | bytes 18878464 | tf_op jit(solution)/shard_map/reduce_sum | solution.py:12
  517.4 11.3 %fusion.119 = bf16[2,512,4,256]{3,1,2,0:T(8,128)(2,1)S(1)} fusion(bf16[1,3072,4,256]{3,2,1,0:T(4,128)(2,1)} %get-tuple-element.17, bf16[2,512,3072]{2,1,0:T(8,128)(2,1)} %get-tuple-element.9, f32[3072]{0:T(1024)S(1)} %bitcast.146, f32[2,512]{1,0:T(2,128)S(1)} %add_rsqrt_fusion.1), kind=kOutput, calls=%fused_computation.129 | convolution fusion | flops 6456082432 | bytes 14696448 | tf_op jit(solution)/shard_map/duo,ojf->dujf/dot_general | solution.py:35
  528.7 6.9 fusion.71
  535.6 6.9 fusion.69
  546.8 5.6 fusion.153
  552.4 14.0 %bitcast_convert_fusion = bf16[2,512,3072]{2,1,0:T(8,128)(2,1)} fusion(bf16[2,4,256,3072]{3,2,1,0:T(8,128)(2,1)} %param.16, bf16[2,512,4,256]{3,1,2,0:T(8,128)(2,1)S(1)} %fusion.119, f32[2,4,512,512]{2,3,1,0:T(8,128)} %get-tuple-element.39, f32[2,4,512]{2,1,0:T(4,128)S(1)} %get-tuple-element.38), kind=kOutput, calls=%fused_computation.68 | convolution fusion | flops 7524581376 | bytes 23085056 | tf_op jit(solution)/shard_map/bqhd,hdm->bqm/dot_general | solution.py:68
  566.4 114.1 %all-reduce.9.cloned.1.call-done = bf16[2,512,3072]{2,1,0:T(8,128)(2,1)} async-done(((bf16[2,512,3072]{2,1,0:T(8,128)(2,1)}), bf16[2,512,3072]{2,1,0:T(8,128)(2,1)}) %all-reduce.9.cloned.1.call-update) | async-done | bytes 6291472 | tf_op jit(solution)/shard_map/psum | solution.py:69
  680.6 10.3 %fusion.54 = (f32[2,512]{1,0:T(2,128)S(1)}, bf16[2,512,3072]{2,1,0:T(8,128)(2,1)}) fusion(bf16[2,512,3072]{2,1,0:T(8,128)(2,1)} %all-reduce.9.cloned.1.call-done, bf16[2,512,3072]{2,1,0:T(8,128)(2,1)} %get-tuple-element.9), kind=kLoop, calls=%fused_computation.64 | loop fusion | flops 22019072 | bytes 18878464 | tf_op jit(solution)/shard_map/reduce_sum | solution.py:12
  690.9 48.7 %fusion.6 = f32[2,512,6144]{2,1,0:T(8,128)} fusion(bf16[2,3072,6144]{2,1,0:T(8,128)(2,1)} %param.17, bf16[2,512,3072]{2,1,0:T(8,128)(2,1)} %get-tuple-element.7, f32[3072]{0:T(1024)S(1)} %bitcast.149, f32[2,512]{1,0:T(2,128)S(1)} %add_rsqrt_fusion), kind=kOutput, calls=%fused_computation.8 | convolution fusion | flops 38667288576 | bytes 69222400 | tf_op jit(solution)/shard_map/bsm,mf->bsf/dot_general | solution.py:48
  739.6 50.1 %fusion.37.clone.7 = bf16[2,512,6144]{2,1,0:T(8,128)(2,1)} fusion(f32[2,512,6144]{2,1,0:T(8,128)} %fusion.6, bf16[2,3072,6144]{2,1,0:T(8,128)(2,1)} %param.18, bf16[2,512,3072]{2,1,0:T(8,128)(2,1)S(1)} %copy-done.2, f32[3072]{0:T(1024)S(1)} %bitcast.150, f32[2,512]{1,0:T(2,128)S(1)} %add_rsqrt_fusion), kind=kOutput, calls=%fused_computation.39.clone.clone.clone.clone.clone.2 | convolution fusion | flops 38730203136 | bytes 81805312 | tf_op jit(solution)/shard_map/bsm,mf->bsf/dot_general | solution.py:49
  789.6 47.6 %fusion.89 = bf16[2,512,3072]{2,1,0:T(8,128)(2,1)} fusion(bf16[2,6144,3072]{2,1,0:T(8,128)(2,1)} %param.19, bf16[2,512,6144]{2,1,0:T(8,128)(2,1)} %fusion.37.clone.7), kind=kOutput, calls=%fused_computation.97 | convolution fusion | flops 38657851392 | bytes 56623104 | tf_op jit(solution)/shard_map/bsf,fm->bsm/dot_general | solution.py:51
  843.1 7.4 copy.24
  854.5 97.0 %all-reduce.11.cloned.1.call-done = bf16[2,512,3072]{2,1,0:T(8,128)(2,1)} async-done(((bf16[2,512,3072]{2,1,0:T(8,128)(2,1)}), bf16[2,512,3072]{2,1,0:T(8,128)(2,1)}) %all-reduce.11.cloned.1.call-update) | async-done | bytes 6291472 | tf_op jit(solution)/shard_map/psum | solution.py:73
  951.5 10.2 %fusion.57 = bf16[2,512,3072]{2,1,0:T(8,128)(2,1)} fusion(bf16[2,512,3072]{2,1,0:T(8,128)(2,1)} %get-tuple-element.7, bf16[2,512,3072]{2,1,0:T(8,128)(2,1)} %all-reduce.11.cloned.1.call-done), kind=kLoop, calls=%fused_computation.67 | loop fusion | flops 12582912 | bytes 18874368 | tf_op jit(solution)/shard_map/convert_element_type | solution.py:74
  (94 shorter events, 29.1 us)
Async XLA Ops:
  7.2 5.0 copy-start.21
  7.2 228.9 %all-reduce.5.cloned.1.call-start = ((), (), s32[]{:S(2)}) async-start(), calls=%async_computation | async-start | bytes 12582912 | tf_op jit(solution)/shard_map/psum | solution.py:69
  13.8 79.6 %copy-start.14 = (f32[512,128]{0,1:T(8,128)}, f32[512,128]{0,1:T(8,128)S(1)}, u32[]{:S(2)}) copy-start(f32[512,128]{0,1:T(8,128)S(1)} %get-tuple-element.34) | copy-start | bytes 786436
  13.8 79.6 %copy-start.16 = (f32[512,128]{0,1:T(8,128)}, f32[512,128]{0,1:T(8,128)S(1)}, u32[]{:S(2)}) copy-start(f32[512,128]{0,1:T(8,128)S(1)} %get-tuple-element.35) | copy-start | bytes 786436
  48.5 21.7 %slice-start = ((s8[6291456]{0:T(1024)(128)(4,1)}), s8[2097152]{0:T(1024)(128)(4,1)S(1)}, s32[]{:S(2)}) async-start(s8[6291456]{0:T(1024)(128)(4,1)} %bitcast.138), calls=%async_computation.4 | async-start | bytes 4194304
  59.2 11.0 %slice-start.1 = ((s8[6291456]{0:T(1024)(128)(4,1)}), s8[4194304]{0:T(1024)(128)(4,1)S(1)}, s32[]{:S(2)}) async-start(s8[6291456]{0:T(1024)(128)(4,1)} %bitcast.138), calls=%async_computation.5 | async-start | bytes 8388608
  59.2 11.0 %copy-start.11 = (bf16[1,3072,4,256]{1,3,2,0:T(8,128)(2,1)S(1)}, bf16[1,3072,4,256]{1,3,2,0:T(8,128)(2,1)}, u32[]{:S(2)}) copy-start(bf16[1,3072,4,256]{1,3,2,0:T(8,128)(2,1)} %copy.35) | copy-start | bytes 18874372
  59.2 19.5 %slice-start.2 = ((s8[12582912]{0:T(1024)(128)(4,1)}), s8[4194304]{0:T(1024)(128)(4,1)S(1)}, s32[]{:S(2)}) async-start(s8[12582912]{0:T(1024)(128)(4,1)} %bitcast.140), calls=%async_computation.6 | async-start | bytes 8388608
  59.2 19.5 %slice-start.3 = ((s8[12582912]{0:T(1024)(128)(4,1)}), s8[4194304]{0:T(1024)(128)(4,1)S(1)}, s32[]{:S(2)}) async-start(s8[12582912]{0:T(1024)(128)(4,1)} %bitcast.140), calls=%async_computation.7 | async-start | bytes 8388608
  70.3 8.5 slice-start.4
  93.4 6.6 copy-start.12
  97.1 1.3 copy-start.5
  99.9 5.4 copy-start.18
  119.3 387.6 %all-reduce.7.cloned.1.call-start = ((), (), s32[]{:S(2)}) async-start(), calls=%async_computation.1 | async-start | bytes 12582912 | tf_op jit(solution)/shard_map/psum | solution.py:73
  246.3 48.7 %copy-start.1 = (bf16[2,512,3072]{2,1,0:T(8,128)(2,1)S(1)}, bf16[2,512,3072]{2,1,0:T(8,128)(2,1)}, u32[]{:S(2)}) copy-start(bf16[2,512,3072]{2,1,0:T(8,128)(2,1)} %get-tuple-element.11) | copy-start | bytes 18874372
  392.7 287.9 %all-reduce.9.cloned.1.call-start = ((), (), s32[]{:S(2)}) async-start(), calls=%async_computation.2 | async-start | bytes 12582912 | tf_op jit(solution)/shard_map/psum | solution.py:69
  414.0 103.3 %copy-start.23 = (f32[1,3072]{1,0:T(1,128)S(1)}, f32[1,3072]{1,0:T(1,128)}, u32[]{:S(2)}) copy-start(f32[1,3072]{1,0:T(1,128)} %get-tuple-element.32) | copy-start | bytes 36868
  506.9 21.7 %slice-start.5 = ((s8[6291456]{0:T(1024)(128)(4,1)}), s8[2097152]{0:T(1024)(128)(4,1)S(1)}, s32[]{:S(2)}) async-start(s8[6291456]{0:T(1024)(128)(4,1)} %bitcast.142), calls=%async_computation.9 | async-start | bytes 4194304
  517.4 11.3 %copy-start = (bf16[2,512,3072]{2,1,0:T(8,128)(2,1)S(1)}, bf16[2,512,3072]{2,1,0:T(8,128)(2,1)}, u32[]{:S(2)}) copy-start(bf16[2,512,3072]{2,1,0:T(8,128)(2,1)} %get-tuple-element.9) | copy-start | bytes 18874372
  517.4 11.3 %slice-start.6 = ((s8[6291456]{0:T(1024)(128)(4,1)}), s8[4194304]{0:T(1024)(128)(4,1)S(1)}, s32[]{:S(2)}) async-start(s8[6291456]{0:T(1024)(128)(4,1)} %bitcast.142), calls=%async_computation.10 | async-start | bytes 8388608
  528.7 23.7 %copy-start.20 = (bf16[2,512,4,256]{3,1,2,0:T(8,128)(2,1)}, bf16[2,512,4,256]{3,1,2,0:T(8,128)(2,1)S(1)}, u32[]{:S(2)}) copy-start(bf16[2,512,4,256]{3,1,2,0:T(8,128)(2,1)S(1)} %fusion.119) | copy-start | bytes 6291460
  528.7 6.9 copy-start.10
  535.6 6.9 copy-start.15
  535.6 6.9 copy-start.17
  544.0 1.3 copy-start.9
  545.3 1.6 copy-start.13
  566.4 124.5 %copy-start.24 = (f32[1,3072]{1,0:T(1,128)S(1)}, f32[1,3072]{1,0:T(1,128)}, u32[]{:S(2)}) copy-start(f32[1,3072]{1,0:T(1,128)} %get-tuple-element.30) | copy-start | bytes 36868
  566.4 385.1 %all-reduce.11.cloned.1.call-start = ((), (), s32[]{:S(2)}) async-start(), calls=%async_computation.3 | async-start | bytes 12582912 | tf_op jit(solution)/shard_map/psum | solution.py:73
  690.9 48.7 %copy-start.2 = (bf16[2,512,3072]{2,1,0:T(8,128)(2,1)S(1)}, bf16[2,512,3072]{2,1,0:T(8,128)(2,1)}, u32[]{:S(2)}) copy-start(bf16[2,512,3072]{2,1,0:T(8,128)(2,1)} %get-tuple-element.7) | copy-start | bytes 18874372
  837.3 1.5 copy-start.6
  837.3 1.9 copy-start.8
  843.1 7.4 copy-start.19
  (4 other events, 3.9 us)
Sparse Core Ops, SparseCore 0:
  119.4 116.6 all-reduce.4
  392.8 114.0 all-reduce.6
  566.5 114.0 all-reduce.8
  837.4 114.0 all-reduce.10
where the time goes:
time: 972 us; the launch traced here: 968 us
  waiting for transfers between devices  420 us (43%)
  matrix products  377 us (39%)
  local copies, waits for them, and re-layouts  85.1 us (9%)
  other arithmetic  72.7 us (7%)
  between operations  14.5 us (1%)
    psum x4, waiting for transfers between devices, shard_body(): summed = lax.psum(part_sum, 'tp')  419 us
    dot_general x2, matrix products, mlp_partial(): jnp.einsum('bsm,mf->bsf', normed, w_up, preferred_element_type=jnp.float32)  100 us
    dot_general x2, matrix products, mlp_partial(): jnp.einsum('bsm,mf->bsf', normed, w_gate, preferred_element_type=jnp.floa...  97.4 us
    dot_general x2, matrix products, mlp_partial(): jnp.einsum('bsf,fm->bsm', hidden_act, w_down, preferred_element_type=jnp....  95.3 us
    unnamed x69, local copies, waits for them, and re-layouts  55.2 us
    reduce_sum x4, other arithmetic, rms_norm(): mean_sq = jnp.mean(x_f32 * x_f32, axis=-1, keepdims=True)  35 us
    dot_general x2, matrix products, shard_body(): jnp.einsum('bqhd,hdm->bqm', attn_out, w_out[layer_idx], preferred_element...  27.9 us
    dot_general x2, matrix products, attention(): jnp.einsum('duo,ojf->dujf', normed, w_value, preferred_element_type=jnp.f...  19.7 us
  transfers between devices with their start and end apart: 4, of which 4 were waited for; matrix products, arithmetic and copies ran while one was open for 4% of the time, Pallas kernels for 0%

commit v1 on v0

v1 whole, which is shorter than its diff:
```python
import functools

import jax
import jax.numpy as jnp
from jax import lax
from jax.experimental import pallas as pl
from jax.experimental.pallas import tpu as pltpu
from jax.sharding import PartitionSpec as P

RMS_EPS = 1e-6
ROPE_BASE = 10000.0
CORE_SWAP = [(0, 1), (1, 0), (2, 3), (3, 2)]
CHIP_SWAP = [(0, 2), (1, 3), (2, 0), (3, 1)]


def rms_norm(x_in, norm_gain):
    x_f32 = x_in.astype(jnp.float32)
    mean_sq = jnp.mean(x_f32 * x_f32, axis=-1, keepdims=True)
    return (x_f32 * lax.rsqrt(mean_sq + RMS_EPS) * (1.0 + norm_gain)).astype(jnp.bfloat16)


def rope_tables(seq_len, head_dim):
    half_dim = head_dim // 2
    inv_freq = ROPE_BASE ** (-jnp.arange(half_dim, dtype=jnp.float32) * (2.0 / head_dim))
    angles = jnp.arange(seq_len, dtype=jnp.float32)[:, None] * inv_freq[None, :]
    return jnp.cos(angles), jnp.sin(angles)


def attn_kernel(len_ref, q_ref, k_ref, v_ref, cos_ref, sin_ref, o_ref, kc_ref):
    seq, dim = q_ref.shape[1:]
    half = dim // 2
    cos_t, sin_t = cos_ref[...], sin_ref[...]

    def rope(ref):
        lo, hi = ref[0, :, :half], ref[0, :, half:]
        return jnp.concatenate([lo * cos_t - hi * sin_t, hi * cos_t + lo * sin_t], axis=-1)

    qr = (rope(q_ref) * (dim ** -0.5)).astype(jnp.bfloat16)
    kr = rope(k_ref).astype(jnp.bfloat16)
    kc_ref[0] = kr
    scores = lax.dot_general(qr, kr, (((1,), (1,)), ((), ())), preferred_element_type=jnp.float32)
    row = lax.broadcasted_iota(jnp.int32, (seq, seq), 0)
    col = lax.broadcasted_iota(jnp.int32, (seq, seq), 1)
    scores = jnp.where((col <= row) & (col < len_ref[0]), scores, -1e30)
    p = jnp.exp(scores - jnp.max(scores, axis=-1, keepdims=True))
    p = p / jnp.sum(p, axis=-1, keepdims=True)
    o = jnp.dot(p.astype(jnp.bfloat16), v_ref[0], preferred_element_type=jnp.float32)
    o_ref[...] = o.astype(jnp.bfloat16)


def attention(length, q, k, v, cos_t, sin_t):
    heads, seq, dim = q.shape
    per_head = pl.BlockSpec((1, seq, dim), lambda h: (h, 0, 0))
    table = pl.BlockSpec((seq, dim // 2), lambda h: (0, 0))
    return pl.pallas_call(
        attn_kernel,
        grid=(heads,),
        in_specs=[pl.BlockSpec(memory_space=pltpu.SMEM), per_head, per_head, per_head, table, table],
        out_specs=[pl.BlockSpec((seq, dim), lambda h: (0, h)), per_head],
        out_shape=[
            jax.ShapeDtypeStruct((seq, heads * dim), jnp.bfloat16),
            jax.ShapeDtypeStruct((heads, seq, dim), jnp.bfloat16),
        ],
        cost_estimate=pl.CostEstimate(
            flops=4 * heads * seq * seq * dim, bytes_accessed=12 * heads * seq * dim, transcendentals=heads * seq * seq
        ),
    )(length, q, k, v, cos_t, sin_t)


def reduce_into(x, part, core):
    half = x.shape[0] // 2
    mine = lax.dynamic_slice_in_dim(part, core * half, half, 0)
    other = lax.dynamic_slice_in_dim(part, (1 - core) * half, half, 0)
    got = lax.ppermute(other, "tp", CORE_SWAP)
    chip_sum = (mine.astype(jnp.float32) + got.astype(jnp.float32)).astype(jnp.bfloat16)
    far_sum = lax.ppermute(chip_sum, "tp", CHIP_SWAP)
    x_mine = lax.dynamic_slice_in_dim(x, core * half, half, 0)
    x_mine = (x_mine.astype(jnp.float32) + (chip_sum.astype(jnp.float32) + far_sum.astype(jnp.float32))).astype(jnp.bfloat16)
    x_other = lax.ppermute(x_mine, "tp", CORE_SWAP)
    return jnp.where(core == 0, jnp.concatenate([x_mine, x_other]), jnp.concatenate([x_other, x_mine]))


def solution(mesh):
    head_cols = P(None, None, "tp", None)
    head_rows = P(None, "tp", None, None)
    ff_cols = P(None, None, "tp")
    ff_rows = P(None, "tp", None)
    f32 = jnp.float32

    def shard_body(hidden, lengths, w_query, w_key, w_value, w_out, w_gate, w_up, w_down, norm_attn, norm_mlp):
        core = lax.axis_index("tp") % 2
        n_layers, _, heads, dim = w_query.shape
        prompts, seq, model = hidden.shape
        cos_t, sin_t = rope_tables(seq, dim)

        def attn_part(x, b, l):
            a = rms_norm(x, norm_attn[l])
            q = jnp.einsum("so,ojf->jsf", a, w_query[l], preferred_element_type=f32)
            k = jnp.einsum("so,ojf->jsf", a, w_key[l], preferred_element_type=f32)
            v = jnp.einsum("so,ojf->jsf", a, w_value[l], preferred_element_type=f32).astype(jnp.bfloat16)
            o, kr = attention(lengths[b][None], q, k, v, cos_t, sin_t)
            part = jnp.dot(o, w_out[l].reshape(heads * dim, model), preferred_element_type=f32).astype(jnp.bfloat16)
            return part, kr, v

        def mlp_part(x, l):
            a = rms_norm(x, norm_mlp[l])
            g = jnp.dot(a, w_gate[l], preferred_element_type=f32)
            u = jnp.dot(a, w_up[l], preferred_element_type=f32)
            m = (jax.nn.gelu(g, approximate=True) * u).astype(jnp.bfloat16)
            return jnp.dot(m, w_down[l], preferred_element_type=f32).astype(jnp.bfloat16)

        xs = [hidden[b] for b in range(prompts)]
        keys, values = [], []
        for l in range(n_layers):
            for b in range(prompts):
                part, kr, v = attn_part(xs[b], b, l)
                keys.append(kr)
                values.append(v)
                xs[b] = reduce_into(xs[b], part, core)
            for b in range(prompts):
                xs[b] = reduce_into(xs[b], mlp_part(xs[b], l), core)
        cache = lambda parts: jnp.stack(parts).reshape(n_layers, prompts, heads, seq, dim)
        return jnp.stack(xs), cache(keys), cache(values)

    return jax.shard_map(
        shard_body,
        mesh=mesh,
        in_specs=(P("dp"), P("dp"), head_cols, head_cols, head_cols, head_rows, ff_cols, ff_cols, ff_rows, P(), P()),
        out_specs=(P("dp"), P(None, "dp", "tp"), P(None, "dp", "tp")),
        check_vma=False,
    )
```

time: 972 us -> 842 us (0.87)
  waiting for transfers between devices: 420 us -> 264 us
  matrix products: 377 us -> 419 us
  local copies, waits for them, and re-layouts: 85.1 us -> 49.1 us
  Pallas kernels: 0 us -> 29.9 us
  other arithmetic: 72.7 us -> 55.3 us
  starting transfers between devices: 0.16 us -> 13.1 us
  between operations: 14.5 us -> 2 us
    psum x4 -> x0, waiting for transfers between devices: 419 us -> none  [shard_body(): summed = lax.psum(part_sum, 'tp')]
    ppermute x0 -> x24, waiting for transfers between devices: none -> 264 us  [the longest x8 264 us: reduce_into(): far_sum = lax.ppermute(chip_sum, 'tp', CHIP_SWAP)]
    unnamed x69 -> x110, local copies, waits for them, and re-layouts: 55.2 us -> 11.8 us
    dot_general x16 -> x28, matrix products: 377 us -> 419 us  [the longest x4 118 us: mlp_part(): u = jnp.dot(a, w_up[l], preferred_element_type=f32)]
    pallas_call x0 -> x4, Pallas kernels: none -> 29.9 us  [attention(): pl.pallas_call(attn_kernel, grid=(heads,), in_specs=[pl.BlockSpec(memory_...]
    reduce_sum x4 -> x7, other arithmetic: 35 us -> 20.1 us  [rms_norm(): mean_sq = jnp.mean(x_f32 * x_f32, axis=-1, keepdims=True)]
    ppermute x0 -> x24, starting transfers between devices: none -> 13.1 us  [the longest x8 9.44 us: reduce_into(): far_sum = lax.ppermute(chip_sum, 'tp', CHIP_SWAP)]
    convert_element_type x1 -> x16, other arithmetic: 10.2 us -> 21.4 us  [the longest x8 12.8 us: reduce_into(): (mine.astype(jnp.float32) + got.astype(jnp.float32)).astype(jnp.bfloat16)]
  transfers between devices with their start and end apart: 4 -> 24, of which waited for: 4 -> 8; matrix products, arithmetic and copies ran while one was open for 4% -> 40% of each run, Pallas kernels for 0% -> 2%
where the time goes in v1:
time: 842 us; the launch traced here: 833 us
  matrix products  419 us (50%)
  waiting for transfers between devices  264 us (31%)
  other arithmetic  55.3 us (7%)
  local copies, waits for them, and re-layouts  49.1 us (6%)
  Pallas kernels  29.9 us (4%)
  starting transfers between devices  13.1 us (2%)
    ppermute x8, waiting for transfers between devices, reduce_into(): far_sum = lax.ppermute(chip_sum, 'tp', CHIP_SWAP)  264 us
    dot_general x4, matrix products, mlp_part(): u = jnp.dot(a, w_up[l], preferred_element_type=f32)  118 us
    dot_general x4, matrix products, mlp_part(): g = jnp.dot(a, w_gate[l], preferred_element_type=f32)  109 us
    dot_general x4, matrix products, mlp_part(): jnp.dot(m, w_down[l], preferred_element_type=f32).astype(jnp.bfloat16)  103 us
    pallas_call x4, Pallas kernels, attention(): pl.pallas_call(attn_kernel, grid=(heads,), in_specs=[pl.BlockSpec(memory_...  29.9 us
    dot_general x4, matrix products, attn_part(): jnp.dot(o, w_out[l].reshape(heads * dim, model), preferred_element_type=f32)  26.4 us
    dot_general x4, matrix products, attn_part(): q = jnp.einsum('so,ojf->jsf', a, w_query[l], preferred_element_type=f32)  25.3 us
    reduce_sum x7, other arithmetic, rms_norm(): mean_sq = jnp.mean(x_f32 * x_f32, axis=-1, keepdims=True)  20.1 us
  transfers between devices with their start and end apart: 24, of which 8 were waited for; matrix products, arithmetic and copies ran while one was open for 40% of the time, Pallas kernels for 2%

profile of v1, /device:TPU:0, one launch (start us, length us, event | category | flops | bytes accessed | tf_op | source)
XLA Modules:
  0.0 832.7 jit_solution(15456573796993876851)
XLA Ops:
  8.0 11.6 %fusion.223 = (bf16[1,3072,4,256]{3,2,1,0:T(4,128)(2,1)S(1)}, bf16[1,3072,4,256]{3,2,1,0:T(4,128)(2,1)}) fusion(bf16[2,3072,4,256]{3,2,1,0:T(4,128)(2,1)} %param.13), kind=kLoop, calls=%fused_computation.246 | loop fusion | bytes 25165824 | tf_op jit(solution)/shard_map/slice | solution.py:98
  19.7 6.1 fusion.222
  51.1 7.6 shard_map.132
  58.8 6.7 convolution_convert_fusion.1
  67.9 8.1 fusion.172.q_ref
  85.3 7.6 shard_map.130
  92.9 6.5 convolution_convert_fusion.3
  112.0 31.6 %collective-permute-done.13 = bf16[256,3072]{1,0:T(8,128)(2,1)S(1)} collective-permute-done((bf16[256,3072]{1,0:T(8,128)(2,1)S(1)}, bf16[256,3072]{1,0:T(8,128)(2,1)S(1)}, u32[]{:S(2)}, u32[]{:S(2)}) %collective-permute-start.13) | collective-permute-done | bytes 1572896 | tf_op jit(solution)/shard_map/ppermute | solution.py:76
  144.5 32.7 %collective-permute-done.1 = bf16[256,3072]{1,0:T(8,128)(2,1)S(1)} collective-permute-done((bf16[256,3072]{1,0:T(8,128)(2,1)S(1)}, bf16[256,3072]{1,0:T(8,128)(2,1)S(1)}, u32[]{:S(2)}, u32[]{:S(2)}) %collective-permute-start.1) | collective-permute-done | bytes 1572896 | tf_op jit(solution)/shard_map/ppermute | solution.py:76
  187.9 27.6 %fusion.22 = f32[512,6144]{1,0:T(8,128)} fusion(bf16[2,3072,6144]{2,1,0:T(8,128)(2,1)} %param.17, bf16[512,3072]{1,0:T(8,128)(2,1)} %get-tuple-element.26, f32[3072]{0:T(1024)S(1)} %bitcast.282, f32[512]{0:T(512)S(1)} %add_rsqrt_fusion.6), kind=kOutput, calls=%fused_computation.22 | convolution fusion | flops 19333644288 | bytes 53491712 | tf_op jit(solution)/shard_map/dot_general | solution.py:107
  215.5 30.3 %fusion.44.clone.7 = bf16[512,6144]{1,0:T(8,128)(2,1)} fusion(f32[512,6144]{1,0:T(8,128)} %fusion.22, bf16[2,3072,6144]{2,1,0:T(8,128)(2,1)} %param.18, bf16[512,3072]{1,0:T(8,128)(2,1)} %get-tuple-element.26, f32[3072]{0:T(1024)S(1)} %bitcast.283, f32[512]{0:T(512)S(1)} %add_rsqrt_fusion.6), kind=kOutput, calls=%fused_computation.48.clone.clone.clone.clone.clone.2 | convolution fusion | flops 19365101568 | bytes 59783168 | tf_op jit(solution)/shard_map/dot_general | solution.py:108
  245.8 25.7 %fusion.140 = bf16[512,3072]{1,0:T(8,128)(2,1)S(1)} fusion(bf16[2,6144,3072]{2,1,0:T(8,128)(2,1)} %param.19, bf16[512,6144]{1,0:T(8,128)(2,1)} %fusion.44.clone.7), kind=kOutput, calls=%fused_computation.155 | convolution fusion | flops 19328925696 | bytes 47185920 | tf_op jit(solution)/shard_map/dot_general | solution.py:110
  274.9 26.9 %fusion.20 = f32[512,6144]{1,0:T(8,128)} fusion(bf16[2,3072,6144]{2,1,0:T(8,128)(2,1)} %param.17, bf16[512,3072]{1,0:T(8,128)(2,1)S(1)} %get-tuple-element.32, f32[512]{0:T(512)S(1)} %add_rsqrt_fusion.2, f32[3072]{0:T(1024)S(1)} %bitcast.284), kind=kOutput, calls=%fused_computation.20 | convolution fusion | flops 19333644288 | bytes 53491712 | tf_op jit(solution)/shard_map/dot_general | solution.py:107
  301.8 29.3 %fusion.62.clone.7 = bf16[512,6144]{1,0:T(8,128)(2,1)} fusion(f32[512,6144]{1,0:T(8,128)} %fusion.20, bf16[2,3072,6144]{2,1,0:T(8,128)(2,1)} %param.18, bf16[512,3072]{1,0:T(8,128)(2,1)S(1)} %get-tuple-element.32, f32[512]{0:T(512)S(1)} %add_rsqrt_fusion.2, f32[3072]{0:T(1024)S(1)} %bitcast.285), kind=kOutput, calls=%fused_computation.66.clone.clone.clone.clone.clone.2 | convolution fusion | flops 19365101568 | bytes 59783168 | tf_op jit(solution)/shard_map/dot_general | solution.py:108
  331.1 25.9 %fusion.145 = bf16[512,3072]{1,0:T(8,128)(2,1)S(1)} fusion(bf16[2,6144,3072]{2,1,0:T(8,128)(2,1)} %param.19, bf16[512,6144]{1,0:T(8,128)(2,1)} %fusion.62.clone.7), kind=kOutput, calls=%fused_computation.156 | convolution fusion | flops 19328925696 | bytes 47185920 | tf_op jit(solution)/shard_map/dot_general | solution.py:110
  363.6 34.6 %collective-permute-done.4 = bf16[256,3072]{1,0:T(8,128)(2,1)S(1)} collective-permute-done((bf16[256,3072]{1,0:T(8,128)(2,1)S(1)}, bf16[256,3072]{1,0:T(8,128)(2,1)S(1)}, u32[]{:S(2)}, u32[]{:S(2)}) %collective-permute-start.4) | collective-permute-done | bytes 1572896 | tf_op jit(solution)/shard_map/ppermute | solution.py:76
  399.0 31.9 %collective-permute-done.16 = bf16[256,3072]{1,0:T(8,128)(2,1)S(1)} collective-permute-done((bf16[256,3072]{1,0:T(8,128)(2,1)S(1)}, bf16[256,3072]{1,0:T(8,128)(2,1)S(1)}, u32[]{:S(2)}, u32[]{:S(2)}) %collective-permute-start.16) | collective-permute-done | bytes 1572896 | tf_op jit(solution)/shard_map/ppermute | solution.py:76
  458.4 7.4 shard_map.131
  465.8 6.7 convolution_convert_fusion.2
  475.9 7.6 fusion.169.q_ref
  483.5 7.2 shard_map.133
  490.7 6.5 convolution_convert_fusion
  503.9 34.6 %collective-permute-done.7 = bf16[256,3072]{1,0:T(8,128)(2,1)S(1)} collective-permute-done((bf16[256,3072]{1,0:T(8,128)(2,1)S(1)}, bf16[256,3072]{1,0:T(8,128)(2,1)S(1)}, u32[]{:S(2)}, u32[]{:S(2)}) %collective-permute-start.7) | collective-permute-done | bytes 1572896 | tf_op jit(solution)/shard_map/ppermute | solution.py:76
  539.3 32.0 %collective-permute-done.19 = bf16[256,3072]{1,0:T(8,128)(2,1)S(1)} collective-permute-done((bf16[256,3072]{1,0:T(8,128)(2,1)S(1)}, bf16[256,3072]{1,0:T(8,128)(2,1)S(1)}, u32[]{:S(2)}, u32[]{:S(2)}) %collective-permute-start.19) | collective-permute-done | bytes 1572896 | tf_op jit(solution)/shard_map/ppermute | solution.py:76
  574.9 27.8 %fusion.10 = f32[512,6144]{1,0:T(8,128)} fusion(bf16[2,3072,6144]{2,1,0:T(8,128)(2,1)} %param.17, bf16[512,3072]{1,0:T(8,128)(2,1)S(1)} %get-tuple-element.22, f32[3072]{0:T(1024)S(1)} %bitcast.272, f32[512]{0:T(512)S(1)} %add_rsqrt_fusion.4), kind=kOutput, calls=%fused_computation.10 | convolution fusion | flops 19333644288 | bytes 53491712 | tf_op jit(solution)/shard_map/dot_general | solution.py:107
  602.7 29.3 %fusion.53.clone.7 = bf16[512,6144]{1,0:T(8,128)(2,1)} fusion(f32[512,6144]{1,0:T(8,128)} %fusion.10, bf16[2,3072,6144]{2,1,0:T(8,128)(2,1)} %param.18, bf16[512,3072]{1,0:T(8,128)(2,1)S(1)} %get-tuple-element.22, f32[3072]{0:T(1024)S(1)} %bitcast.273, f32[512]{0:T(512)S(1)} %add_rsqrt_fusion.4), kind=kOutput, calls=%fused_computation.57.clone.clone.clone.clone.clone.2 | convolution fusion | flops 19365101568 | bytes 59783168 | tf_op jit(solution)/shard_map/dot_general | solution.py:108
  632.0 25.8 %fusion.150 = bf16[512,3072]{1,0:T(8,128)(2,1)S(1)} fusion(bf16[2,6144,3072]{2,1,0:T(8,128)(2,1)} %param.19, bf16[512,6144]{1,0:T(8,128)(2,1)} %fusion.53.clone.7), kind=kOutput, calls=%fused_computation.157 | convolution fusion | flops 19328925696 | bytes 47185920 | tf_op jit(solution)/shard_map/dot_general | solution.py:110
  663.2 26.7 %fusion.8 = f32[512,6144]{1,0:T(8,128)} fusion(bf16[2,3072,6144]{2,1,0:T(8,128)(2,1)} %param.17, bf16[512,3072]{1,0:T(8,128)(2,1)S(1)} %get-tuple-element.28, f32[512]{0:T(512)S(1)} %add_rsqrt_fusion, f32[3072]{0:T(1024)S(1)} %bitcast.274), kind=kOutput, calls=%fused_computation.8 | convolution fusion | flops 19333644288 | bytes 53491712 | tf_op jit(solution)/shard_map/dot_general | solution.py:107
  689.9 29.5 %fusion.71.clone.7 = bf16[512,6144]{1,0:T(8,128)(2,1)} fusion(f32[512,6144]{1,0:T(8,128)} %fusion.8, bf16[2,3072,6144]{2,1,0:T(8,128)(2,1)} %param.18, bf16[512,3072]{1,0:T(8,128)(2,1)S(1)} %get-tuple-element.28, f32[512]{0:T(512)S(1)} %add_rsqrt_fusion, f32[3072]{0:T(1024)S(1)} %bitcast.275), kind=kOutput, calls=%fused_computation.75.clone.clone.clone.clone.clone.2 | convolution fusion | flops 19365101568 | bytes 59783168 | tf_op jit(solution)/shard_map/dot_general | solution.py:108
  719.4 25.9 %fusion.155 = bf16[512,3072]{1,0:T(8,128)(2,1)S(1)} fusion(bf16[2,6144,3072]{2,1,0:T(8,128)(2,1)} %param.19, bf16[512,6144]{1,0:T(8,128)(2,1)} %fusion.71.clone.7), kind=kOutput, calls=%fused_computation.158 | convolution fusion | flops 19328925696 | bytes 47185920 | tf_op jit(solution)/shard_map/dot_general | solution.py:110
  751.9 34.6 %collective-permute-done.10 = bf16[256,3072]{1,0:T(8,128)(2,1)S(1)} collective-permute-done((bf16[256,3072]{1,0:T(8,128)(2,1)S(1)}, bf16[256,3072]{1,0:T(8,128)(2,1)S(1)}, u32[]{:S(2)}, u32[]{:S(2)}) %collective-permute-start.10) | collective-permute-done | bytes 1572896 | tf_op jit(solution)/shard_map/ppermute | solution.py:76
  787.4 32.0 %collective-permute-done.22 = bf16[256,3072]{1,0:T(8,128)(2,1)S(1)} collective-permute-done((bf16[256,3072]{1,0:T(8,128)(2,1)S(1)}, bf16[256,3072]{1,0:T(8,128)(2,1)S(1)}, u32[]{:S(2)}, u32[]{:S(2)}) %collective-permute-start.22) | collective-permute-done | bytes 1572896 | tf_op jit(solution)/shard_map/ppermute | solution.py:76
  (222 shorter events, 146.3 us)
Async XLA Ops:
  66.8 36.5 %collective-permute-start.12 = (bf16[256,3072]{1,0:T(8,128)(2,1)}, bf16[256,3072]{1,0:T(8,128)(2,1)}, u32[]{:S(2)}, u32[]{:S(2)}) collective-permute-start(bf16[256,3072]{1,0:T(8,128)(2,1)} %constant_dynamic-slice_fusion.3), channel_id=1, source_target_pairs={{0,1},{1,0},{2,3},{3,2},{4,5},{5,4},{6,7},{7,6}} | collective-permute-start | bytes 4718600 | tf_op jit(solution)/shard_map/ppermute | solution.py:74
  102.4 6.0 collective-permute-start
  105.9 37.8 %collective-permute-start.13 = (bf16[256,3072]{1,0:T(8,128)(2,1)S(1)}, bf16[256,3072]{1,0:T(8,128)(2,1)S(1)}, u32[]{:S(2)}, u32[]{:S(2)}) collective-permute-start(bf16[256,3072]{1,0:T(8,128)(2,1)S(1)} %add_convert_fusion.6), channel_id=1, source_target_pairs={{0,2},{1,3},{2,0},{3,1},{4,6},{5,7},{6,4},{7,5}} | collective-permute-start | bytes 4718600 | tf_op jit(solution)/shard_map/ppermute | solution.py:76
  110.8 66.3 %collective-permute-start.1 = (bf16[256,3072]{1,0:T(8,128)(2,1)S(1)}, bf16[256,3072]{1,0:T(8,128)(2,1)S(1)}, u32[]{:S(2)}, u32[]{:S(2)}) collective-permute-start(bf16[256,3072]{1,0:T(8,128)(2,1)S(1)} %add_convert_fusion.13), channel_id=1, source_target_pairs={{0,2},{1,3},{2,0},{3,1},{4,6},{5,7},{6,4},{7,5}} | collective-permute-start | bytes 4718600 | tf_op jit(solution)/shard_map/ppermute | solution.py:76
  144.4 35.3 %copy-start.9 = (bf16[256,3072]{1,0:T(8,128)(2,1)}, bf16[256,3072]{1,0:T(8,128)(2,1)S(1)}, u32[]{:S(2)}) copy-start(bf16[256,3072]{1,0:T(8,128)(2,1)S(1)} %fusion.164) | copy-start | bytes 4718596
  144.4 34.6 %copy-start.27 = (f32[2,3072]{1,0:T(2,128)S(1)}, f32[2,3072]{1,0:T(2,128)}, u32[]{:S(2)}) copy-start(f32[2,3072]{1,0:T(2,128)} %param.21) | copy-start | bytes 73732
  144.4 35.3 %collective-permute-start.14 = (bf16[256,3072]{1,0:T(8,128)(2,1)S(1)}, bf16[256,3072]{1,0:T(8,128)(2,1)}, u32[]{:S(2)}, u32[]{:S(2)}) collective-permute-start(bf16[256,3072]{1,0:T(8,128)(2,1)S(1)} %fusion.164), channel_id=1, source_target_pairs={{0,1},{1,0},{2,3},{3,2},{4,5},{5,4},{6,7},{7,6}} | collective-permute-start | bytes 4718600 | tf_op jit(solution)/shard_map/ppermute | solution.py:79
  179.1 4.2 collective-permute-start.2
  274.4 82.8 %collective-permute-start.3 = (bf16[256,3072]{1,0:T(8,128)(2,1)}, bf16[256,3072]{1,0:T(8,128)(2,1)}, u32[]{:S(2)}, u32[]{:S(2)}) collective-permute-start(bf16[256,3072]{1,0:T(8,128)(2,1)} %constant_dynamic-slice_fusion.6), channel_id=1, source_target_pairs={{0,1},{1,0},{2,3},{3,2},{4,5},{5,4},{6,7},{7,6}} | collective-permute-start | bytes 4718600 | tf_op jit(solution)/shard_map/ppermute | solution.py:74
  357.1 41.1 %copy-start.5 = (bf16[512,3072]{1,0:T(8,128)(2,1)S(1)}, bf16[512,3072]{1,0:T(8,128)(2,1)}, u32[]{:S(2)}) copy-start(bf16[512,3072]{1,0:T(8,128)(2,1)} %get-tuple-element.26) | copy-start | bytes 9437188
  357.1 5.5 collective-permute-start.15
  360.9 37.3 %collective-permute-start.4 = (bf16[256,3072]{1,0:T(8,128)(2,1)S(1)}, bf16[256,3072]{1,0:T(8,128)(2,1)S(1)}, u32[]{:S(2)}, u32[]{:S(2)}) collective-permute-start(bf16[256,3072]{1,0:T(8,128)(2,1)S(1)} %add_convert_fusion.12), channel_id=1, source_target_pairs={{0,2},{1,3},{2,0},{3,1},{4,6},{5,7},{6,4},{7,5}} | collective-permute-start | bytes 4718600 | tf_op jit(solution)/shard_map/ppermute | solution.py:76
  363.2 67.7 %collective-permute-start.16 = (bf16[256,3072]{1,0:T(8,128)(2,1)S(1)}, bf16[256,3072]{1,0:T(8,128)(2,1)S(1)}, u32[]{:S(2)}, u32[]{:S(2)}) collective-permute-start(bf16[256,3072]{1,0:T(8,128)(2,1)S(1)} %add_convert_fusion.5), channel_id=1, source_target_pairs={{0,2},{1,3},{2,0},{3,1},{4,6},{5,7},{6,4},{7,5}} | collective-permute-start | bytes 4718600 | tf_op jit(solution)/shard_map/ppermute | solution.py:76
  398.2 35.4 %slice-start.17 = ((s8[6291456]{0:T(1024)(128)(4,1)}), s8[4194304]{0:T(1024)(128)(4,1)S(1)}, s32[]{:S(2)}) async-start(s8[6291456]{0:T(1024)(128)(4,1)} %bitcast.238), calls=%async_computation.17 | async-start | bytes 8388608
  399.0 34.6 %slice-start.18 = ((s8[6291456]{0:T(1024)(128)(4,1)}), s8[2097152]{0:T(1024)(128)(4,1)S(1)}, s32[]{:S(2)}) async-start(s8[6291456]{0:T(1024)(128)(4,1)} %bitcast.238), calls=%async_computation.18 | async-start | bytes 4194304
  399.0 32.8 %collective-permute-start.5 = (bf16[256,3072]{1,0:T(8,128)(2,1)S(1)}, bf16[256,3072]{1,0:T(8,128)(2,1)S(1)}, u32[]{:S(2)}, u32[]{:S(2)}) collective-permute-start(bf16[256,3072]{1,0:T(8,128)(2,1)S(1)} %add_convert_fusion.11), channel_id=1, source_target_pairs={{0,1},{1,0},{2,3},{3,2},{4,5},{5,4},{6,7},{7,6}} | collective-permute-start | bytes 4718600 | tf_op jit(solution)/shard_map/ppermute | solution.py:79
  431.7 11.2 %collective-permute-start.17 = (bf16[256,3072]{1,0:T(8,128)(2,1)S(1)}, bf16[256,3072]{1,0:T(8,128)(2,1)S(1)}, u32[]{:S(2)}, u32[]{:S(2)}) collective-permute-start(bf16[256,3072]{1,0:T(8,128)(2,1)S(1)} %add_convert_fusion.4), channel_id=1, source_target_pairs={{0,1},{1,0},{2,3},{3,2},{4,5},{5,4},{6,7},{7,6}} | collective-permute-start | bytes 4718600 | tf_op jit(solution)/shard_map/ppermute | solution.py:79
  475.4 22.0 %collective-permute-start.6 = (bf16[256,3072]{1,0:T(8,128)(2,1)}, bf16[256,3072]{1,0:T(8,128)(2,1)}, u32[]{:S(2)}, u32[]{:S(2)}) collective-permute-start(bf16[256,3072]{1,0:T(8,128)(2,1)} %constant_dynamic-slice_fusion.5), channel_id=1, source_target_pairs={{0,1},{1,0},{2,3},{3,2},{4,5},{5,4},{6,7},{7,6}} | collective-permute-start | bytes 4718600 | tf_op jit(solution)/shard_map/ppermute | solution.py:74
  497.4 5.5 collective-permute-start.18
  501.2 37.3 %collective-permute-start.7 = (bf16[256,3072]{1,0:T(8,128)(2,1)S(1)}, bf16[256,3072]{1,0:T(8,128)(2,1)S(1)}, u32[]{:S(2)}, u32[]{:S(2)}) collective-permute-start(bf16[256,3072]{1,0:T(8,128)(2,1)S(1)} %add_convert_fusion.10), channel_id=1, source_target_pairs={{0,2},{1,3},{2,0},{3,1},{4,6},{5,7},{6,4},{7,5}} | collective-permute-start | bytes 4718600 | tf_op jit(solution)/shard_map/ppermute | solution.py:76
  503.5 67.7 %copy-start.2 = (bf16[512,3072]{1,0:T(8,128)(2,1)S(1)}, bf16[512,3072]{1,0:T(8,128)(2,1)}, u32[]{:S(2)}) copy-start(bf16[512,3072]{1,0:T(8,128)(2,1)} %copy-done) | copy-start | bytes 9437188
  503.5 67.7 %collective-permute-start.19 = (bf16[256,3072]{1,0:T(8,128)(2,1)S(1)}, bf16[256,3072]{1,0:T(8,128)(2,1)S(1)}, u32[]{:S(2)}, u32[]{:S(2)}) collective-permute-start(bf16[256,3072]{1,0:T(8,128)(2,1)S(1)} %add_convert_fusion.3), channel_id=1, source_target_pairs={{0,2},{1,3},{2,0},{3,1},{4,6},{5,7},{6,4},{7,5}} | collective-permute-start | bytes 4718600 | tf_op jit(solution)/shard_map/ppermute | solution.py:76
  539.2 33.9 %collective-permute-start.8 = (bf16[256,3072]{1,0:T(8,128)(2,1)S(1)}, bf16[256,3072]{1,0:T(8,128)(2,1)S(1)}, u32[]{:S(2)}, u32[]{:S(2)}) collective-permute-start(bf16[256,3072]{1,0:T(8,128)(2,1)S(1)} %add_convert_fusion.9), channel_id=1, source_target_pairs={{0,1},{1,0},{2,3},{3,2},{4,5},{5,4},{6,7},{7,6}} | collective-permute-start | bytes 4718600 | tf_op jit(solution)/shard_map/ppermute | solution.py:79
  573.2 86.6 %collective-permute-start.20 = (bf16[256,3072]{1,0:T(8,128)(2,1)}, bf16[256,3072]{1,0:T(8,128)(2,1)}, u32[]{:S(2)}, u32[]{:S(2)}) collective-permute-start(bf16[256,3072]{1,0:T(8,128)(2,1)} %add_convert_fusion.2), channel_id=1, source_target_pairs={{0,1},{1,0},{2,3},{3,2},{4,5},{5,4},{6,7},{7,6}} | collective-permute-start | bytes 4718600 | tf_op jit(solution)/shard_map/ppermute | solution.py:79
  659.2 86.4 %collective-permute-start.9 = (bf16[256,3072]{1,0:T(8,128)(2,1)}, bf16[256,3072]{1,0:T(8,128)(2,1)}, u32[]{:S(2)}, u32[]{:S(2)}) collective-permute-start(bf16[256,3072]{1,0:T(8,128)(2,1)} %constant_dynamic-slice_fusion.4), channel_id=1, source_target_pairs={{0,1},{1,0},{2,3},{3,2},{4,5},{5,4},{6,7},{7,6}} | collective-permute-start | bytes 4718600 | tf_op jit(solution)/shard_map/ppermute | solution.py:74
  745.5 41.1 %copy-start.4 = (bf16[512,3072]{1,0:T(8,128)(2,1)S(1)}, bf16[512,3072]{1,0:T(8,128)(2,1)}, u32[]{:S(2)}) copy-start(bf16[512,3072]{1,0:T(8,128)(2,1)} %copy-done.3) | copy-start | bytes 9437188
  745.5 5.5 collective-permute-start.21
  749.2 37.3 %collective-permute-start.10 = (bf16[256,3072]{1,0:T(8,128)(2,1)S(1)}, bf16[256,3072]{1,0:T(8,128)(2,1)S(1)}, u32[]{:S(2)}, u32[]{:S(2)}) collective-permute-start(bf16[256,3072]{1,0:T(8,128)(2,1)S(1)} %add_convert_fusion.8), channel_id=1, source_target_pairs={{0,2},{1,3},{2,0},{3,1},{4,6},{5,7},{6,4},{7,5}} | collective-permute-start | bytes 4718600 | tf_op jit(solution)/shard_map/ppermute | solution.py:76
  751.6 67.8 %collective-permute-start.22 = (bf16[256,3072]{1,0:T(8,128)(2,1)S(1)}, bf16[256,3072]{1,0:T(8,128)(2,1)S(1)}, u32[]{:S(2)}, u32[]{:S(2)}) collective-permute-start(bf16[256,3072]{1,0:T(8,128)(2,1)S(1)} %add_convert_fusion.1), channel_id=1, source_target_pairs={{0,2},{1,3},{2,0},{3,1},{4,6},{5,7},{6,4},{7,5}} | collective-permute-start | bytes 4718600 | tf_op jit(solution)/shard_map/ppermute | solution.py:76
  787.3 32.9 %copy-start.22 = (bf16[4,512,256]{2,1,0:T(8,128)(2,1)S(1)}, bf16[4,512,256]{2,1,0:T(8,128)(2,1)}, u32[]{:S(2)}) copy-start(bf16[4,512,256]{2,1,0:T(8,128)(2,1)} %get-tuple-element.16) | copy-start | bytes 3145732
  787.3 38.9 %collective-permute-start.11 = (bf16[256,3072]{1,0:T(8,128)(2,1)S(1)}, bf16[256,3072]{1,0:T(8,128)(2,1)S(1)}, u32[]{:S(2)}, u32[]{:S(2)}) collective-permute-start(bf16[256,3072]{1,0:T(8,128)(2,1)S(1)} %add_convert_fusion.7), channel_id=1, source_target_pairs={{0,1},{1,0},{2,3},{3,2},{4,5},{5,4},{6,7},{7,6}} | collective-permute-start | bytes 4718600 | tf_op jit(solution)/shard_map/ppermute | solution.py:79
  820.2 7.4 collective-permute-start.23
  (47 other events, 422.6 us)

commit v2 on v1

--- a/solution.py
+++ b/solution.py
@@ -67,6 +67,126 @@
     )(length, q, k, v, cos_t, sin_t)
 
 
+GU_COLS = 512
+DOWN_COLS = 512
+
+
+def norm_rows(x_ref, gain_ref, a_ref):
+    rows = x_ref.shape[0]
+    step = 64
+    gain = 1.0 + gain_ref[...]
+
+    def body(i, _):
+        at = pl.ds(pl.multiple_of(i * step, step), step)
+        x = x_ref[at, :].astype(jnp.float32)
+        mean_sq = jnp.mean(x * x, axis=-1, keepdims=True)
+        a_ref[at, :] = (x * lax.rsqrt(mean_sq + RMS_EPS) * gain).astype(jnp.bfloat16)
+        return 0
+
+    lax.fori_loop(0, rows // step, body, 0)
+
+
+def mlp_kernel(layer, x_hbm, gain_ref, wg_hbm, wu_hbm, wd_hbm, out_ref, x_vm, a_vm, m_vm, wg_vm, wu_vm, wd_vm, g_vm, u_vm, x_sem, g_sem, u_sem, d_sem):
+    model, width = wg_hbm.shape[1:]
+    n_gu, n_down = width // GU_COLS, model // DOWN_COLS
+
+    def gu_copies(t, slot):
+        cols = pl.ds(pl.multiple_of(t * GU_COLS, GU_COLS), GU_COLS)
+        return (
+            pltpu.make_async_copy(wg_hbm.at[layer, :, cols], wg_vm.at[slot], g_sem.at[slot]),
+            pltpu.make_async_copy(wu_hbm.at[layer, :, cols], wu_vm.at[slot], u_sem.at[slot]),
+        )
+
+    def down_copy(t, slot):
+        cols = pl.ds(pl.multiple_of(t * DOWN_COLS, DOWN_COLS), DOWN_COLS)
+        return pltpu.make_async_copy(wd_hbm.at[layer, :, cols], wd_vm.at[slot], d_sem.at[slot])
+
+    x_copy = pltpu.make_async_copy(x_hbm, x_vm, x_sem)
+    x_copy.start()
+    for c in gu_copies(0, 0):
+        c.start()
+    x_copy.wait()
+    norm_rows(x_vm, gain_ref, a_vm)
+
+    def finish(t, slot):
+        cols = pl.ds(pl.multiple_of(t * GU_COLS, GU_COLS), GU_COLS)
+        m_vm[:, cols] = (jax.nn.gelu(g_vm[slot], approximate=True) * u_vm[slot]).astype(jnp.bfloat16)
+
+    def one(t, slot, first):
+        for c in gu_copies(t, slot):
+            c.wait()
+
+        @pl.when(t + 1 < n_gu)
+        def _():
+            for c in gu_copies(t + 1, 1 - slot):
+                c.start()
+
+        if not first:
+            finish(t - 1, 1 - slot)
+        g_vm[slot] = jnp.dot(a_vm[...], wg_vm[slot], preferred_element_type=jnp.float32)
+        u_vm[slot] = jnp.dot(a_vm[...], wu_vm[slot], preferred_element_type=jnp.float32)
+
+    one(0, 0, True)
+    down_copy(0, 0).start()
+
+    def pair(i, _):
+        one(2 * i + 1, 1, False)
+        one(2 * i + 2, 0, False)
+        return 0
+
+    lax.fori_loop(0, (n_gu - 2) // 2, pair, 0)
+    one(n_gu - 1, 1, False)
+    finish(n_gu - 1, 1)
+
+    def down(t, slot):
+        down_copy(t, slot).wait()
+
+        @pl.when(t + 1 < n_down)
+        def _():
+            down_copy(t + 1, 1 - slot).start()
+
+        cols = pl.ds(pl.multiple_of(t * DOWN_COLS, DOWN_COLS), DOWN_COLS)
+        out_ref[:, cols] = jnp.dot(m_vm[...], wd_vm[slot], preferred_element_type=jnp.float32).astype(jnp.bfloat16)
+
+    def down_pair(i, _):
+        down(2 * i, 0)
+        down(2 * i + 1, 1)
+        return 0
+
+    lax.fori_loop(0, n_down // 2, down_pair, 0)
+
+
+def mlp(x, gain, wg, wu, wd, layer):
+    rows, model = x.shape
+    width = wg.shape[2]
+    anywhere = pl.BlockSpec(memory_space=pl.ANY)
+    bf16, f32 = jnp.bfloat16, jnp.float32
+    return pl.pallas_call(
+        functools.partial(mlp_kernel, layer),
+        in_specs=[anywhere, pl.BlockSpec(memory_space=pltpu.VMEM), anywhere, anywhere, anywhere],
+        out_specs=pl.BlockSpec(memory_space=pltpu.VMEM),
+        out_shape=jax.ShapeDtypeStruct((rows, model), bf16),
+        scratch_shapes=[
+            pltpu.VMEM((rows, model), bf16),
+            pltpu.VMEM((rows, model), bf16),
+            pltpu.VMEM((rows, width), bf16),
+            pltpu.VMEM((2, model, GU_COLS), bf16),
+            pltpu.VMEM((2, model, GU_COLS), bf16),
+            pltpu.VMEM((2, width, DOWN_COLS), bf16),
+            pltpu.VMEM((2, rows, GU_COLS), f32),
+            pltpu.VMEM((2, rows, GU_COLS), f32),
+            pltpu.SemaphoreType.DMA,
+            pltpu.SemaphoreType.DMA((2,)),
+            pltpu.SemaphoreType.DMA((2,)),
+            pltpu.SemaphoreType.DMA((2,)),
+        ],
+        compiler_params=pltpu.CompilerParams(vmem_limit_bytes=60 * 1024 * 1024),
+        cost_estimate=pl.CostEstimate(
+            flops=6 * rows * model * width, bytes_accessed=6 * model * width + 4 * rows * model, transcendentals=rows * width
+        ),
+    )(x, gain, wg, wu, wd)
+
+
 def reduce_into(x, part, core):
     half = x.shape[0] // 2
     mine = lax.dynamic_slice_in_dim(part, core * half, half, 0)
@@ -103,11 +223,7 @@
             return part, kr, v
 
         def mlp_part(x, l):
-            a = rms_norm(x, norm_mlp[l])
-            g = jnp.dot(a, w_gate[l], preferred_element_type=f32)
-            u = jnp.dot(a, w_up[l], preferred_element_type=f32)
-            m = (jax.nn.gelu(g, approximate=True) * u).astype(jnp.bfloat16)
-            return jnp.dot(m, w_down[l], preferred_element_type=f32).astype(jnp.bfloat16)
+            return mlp(x, norm_mlp[l][None], w_gate, w_up, w_down, l)
 
         xs = [hidden[b] for b in range(prompts)]
         keys, values = [], []

time: 842 us -> 812 us (0.964)
  matrix products: 419 us -> 88.6 us
  Pallas kernels: 29.9 us -> 329 us
    dot_general x12 -> x0, matrix products: 331 us -> none  [the longest x4 118 us: mlp_part(): u = jnp.dot(a, w_up[l], preferred_element_type=f32)]
    pallas_call x0 -> x4, Pallas kernels: none -> 299 us  [mlp(): pl.pallas_call(functools.partial(mlp_kernel, layer), in_specs=[anywhere,...]
    select_n x2 -> x6, other arithmetic: 2.79 us -> 17.2 us  [reduce_into(): jnp.where(core == 0, jnp.concatenate([x_mine, x_other]), jnp.concatenate(...]
    reduce_sum x7 -> x3, other arithmetic: 20.1 us -> 6.44 us  [rms_norm(): mean_sq = jnp.mean(x_f32 * x_f32, axis=-1, keepdims=True)]
    ppermute x8, waiting for transfers between devices: 264 us -> 255 us  [reduce_into(): far_sum = lax.ppermute(chip_sum, 'tp', CHIP_SWAP)]
  transfers between devices with their start and end apart: 24 -> 24, of which waited for: 8 -> 10; matrix products, arithmetic and copies ran while one was open for 40% -> 13% of each run, Pallas kernels for 2% -> 39%
where the time goes in v2:
time: 812 us; the launch traced here: 802 us
  Pallas kernels  329 us (41%)
  waiting for transfers between devices  256 us (32%)
  matrix products  88.6 us (11%)
  other arithmetic  55.9 us (7%)
  local copies, waits for them, and re-layouts  55.1 us (7%)
  starting transfers between devices  16 us (2%)
    pallas_call x4, Pallas kernels, mlp(): pl.pallas_call(functools.partial(mlp_kernel, layer), in_specs=[anywhere,...  299 us
    ppermute x8, waiting for transfers between devices, reduce_into(): far_sum = lax.ppermute(chip_sum, 'tp', CHIP_SWAP)  255 us
    pallas_call x4, Pallas kernels, attention(): pl.pallas_call(attn_kernel, grid=(heads,), in_specs=[pl.BlockSpec(memory_...  30.3 us
    dot_general x4, matrix products, attn_part(): jnp.dot(o, w_out[l].reshape(heads * dim, model), preferred_element_type=f32)  26.3 us
    dot_general x4, matrix products, attn_part(): q = jnp.einsum('so,ojf->jsf', a, w_query[l], preferred_element_type=f32)  25.3 us
    dot_general x4, matrix products, attn_part(): k = jnp.einsum('so,ojf->jsf', a, w_key[l], preferred_element_type=f32)  19.2 us
    dot_general x4, matrix products, attn_part(): jnp.einsum('so,ojf->jsf', a, w_value[l], preferred_element_type=f32)  17.8 us
    select_n x6, other arithmetic, reduce_into(): jnp.where(core == 0, jnp.concatenate([x_mine, x_other]), jnp.concatenate(...  17.2 us
  transfers between devices with their start and end apart: 24, of which 10 were waited for; matrix products, arithmetic and copies ran while one was open for 13% of the time, Pallas kernels for 39%

profile of v2, /device:TPU:0, one launch (start us, length us, event | category | flops | bytes accessed | tf_op | source)
XLA Modules:
  0.0 802.3 jit_solution(12487360608371848137)
XLA Ops:
  8.1 11.6 %fusion.59 = (bf16[1,3072,4,256]{3,2,1,0:T(4,128)(2,1)S(1)}, bf16[1,3072,4,256]{3,2,1,0:T(4,128)(2,1)}) fusion(bf16[2,3072,4,256]{3,2,1,0:T(4,128)(2,1)} %param.13), kind=kLoop, calls=%fused_computation.108 | loop fusion | bytes 25165824 | tf_op jit(solution)/shard_map/slice | solution.py:218
  19.7 6.1 fusion.58
  25.9 4.8 fusion.36.q_ref
  30.7 4.8 fusion.34.k_ref
  35.5 6.0 fusion.57
  46.1 5.2 fusion.56
  51.3 7.9 shard_map.130
  59.2 6.7 convolution_convert_fusion.3
  68.3 8.1 %fusion.37.q_ref = f32[4,512,256]{2,1,0:T(8,128)} fusion(bf16[1,3072,4,256]{3,2,1,0:T(4,128)(2,1)} %copy-done.10, f32[512]{0:T(512)S(1)} %get-tuple-element.43, f32[3072]{0:T(1024)S(1)} %bitcast.177, bf16[2,512,3072]{2,1,0:T(8,128)(2,1)S(1)} %bitcast.129), kind=kOutput, calls=%fused_computation.82 | convolution fusion | flops 3227516928 | bytes 11548672 | tf_op jit(solution)/shard_map/so,ojf->jsf/dot_general | solution.py:218
  76.4 4.8 fusion.35.k_ref
  85.7 7.4 shard_map.134
  93.1 6.5 convolution_convert_fusion.1
  115.7 28.7 %collective-permute-done.1 = bf16[256,3072]{1,0:T(8,128)(2,1)S(1)} collective-permute-done((bf16[256,3072]{1,0:T(8,128)(2,1)S(1)}, bf16[256,3072]{1,0:T(8,128)(2,1)S(1)}, u32[]{:S(2)}, u32[]{:S(2)}) %collective-permute-start.1) | collective-permute-done | bytes 1572896 | tf_op jit(solution)/shard_map/ppermute | solution.py:196
  147.0 30.5 %collective-permute-done.13 = bf16[256,3072]{1,0:T(8,128)(2,1)} collective-permute-done((bf16[256,3072]{1,0:T(8,128)(2,1)}, bf16[256,3072]{1,0:T(8,128)(2,1)}, u32[]{:S(2)}, u32[]{:S(2)}) %collective-permute-start.13) | collective-permute-done | bytes 1572896 | tf_op jit(solution)/shard_map/ppermute | solution.py:196
  185.7 74.7 %shard_map.131 = bf16[512,3072]{1,0:T(8,128)(2,1)} custom-call(bf16[512,3072]{1,0:T(8,128)(2,1)} %maximum_select_fusion.x_hbm, f32[1,3072]{1,0:T(1,128)} %get-tuple-element.36.gain_ref, bf16[2,3072,6144]{2,1,0:T(8,128)(2,1)} %wg_hbm.7, bf16[2,3072,6144]{2,1,0:T(8,128)(2,1)} %wu_hbm.7, bf16[2,6144,3072]{2,1,0:T(8,128)(2,1)} %wd_hbm.7), custom_call_target="tpu_custom_call" | custom-call | flops 57982058496 | bytes 119537664 | tf_op jit(solution)/shard_map/pallas_call | solution.py:164
  267.2 74.6 %shard_map.135 = bf16[512,3072]{1,0:T(8,128)(2,1)} custom-call(bf16[512,3072]{1,0:T(8,128)(2,1)} %maximum_select_fusion.4.x_hbm, f32[1,3072]{1,0:T(1,128)} %get-tuple-element.36.gain_ref, bf16[2,3072,6144]{2,1,0:T(8,128)(2,1)} %wg_hbm.7, bf16[2,3072,6144]{2,1,0:T(8,128)(2,1)} %wu_hbm.7, bf16[2,6144,3072]{2,1,0:T(8,128)(2,1)} %wd_hbm.7), custom_call_target="tpu_custom_call" | custom-call | flops 57982058496 | bytes 119537664 | tf_op jit(solution)/shard_map/pallas_call | solution.py:164
  349.3 32.8 %collective-permute-done.4 = bf16[256,3072]{1,0:T(8,128)(2,1)S(1)} collective-permute-done((bf16[256,3072]{1,0:T(8,128)(2,1)S(1)}, bf16[256,3072]{1,0:T(8,128)(2,1)S(1)}, u32[]{:S(2)}, u32[]{:S(2)}) %collective-permute-start.4) | collective-permute-done | bytes 1572896 | tf_op jit(solution)/shard_map/ppermute | solution.py:196
  382.9 31.9 %collective-permute-done.16 = bf16[256,3072]{1,0:T(8,128)(2,1)S(1)} collective-permute-done((bf16[256,3072]{1,0:T(8,128)(2,1)S(1)}, bf16[256,3072]{1,0:T(8,128)(2,1)S(1)}, u32[]{:S(2)}, u32[]{:S(2)}) %collective-permute-start.16) | collective-permute-done | bytes 1572896 | tf_op jit(solution)/shard_map/ppermute | solution.py:196
  417.1 4.8 fusion.30.k_ref
  432.2 4.8 fusion.31.k_ref
  437.1 4.8 fusion.33.q_ref
  441.9 7.8 shard_map.136
  449.6 6.5 convolution_convert_fusion
  459.6 7.6 fusion.32.q_ref
  467.2 7.2 shard_map.132
  474.4 6.5 convolution_convert_fusion.2
  487.5 34.6 %collective-permute-done.19 = bf16[256,3072]{1,0:T(8,128)(2,1)S(1)} collective-permute-done((bf16[256,3072]{1,0:T(8,128)(2,1)S(1)}, bf16[256,3072]{1,0:T(8,128)(2,1)S(1)}, u32[]{:S(2)}, u32[]{:S(2)}) %collective-permute-start.19) | collective-permute-done | bytes 1572896 | tf_op jit(solution)/shard_map/ppermute | solution.py:196
  523.0 31.9 %collective-permute-done.7 = bf16[256,3072]{1,0:T(8,128)(2,1)S(1)} collective-permute-done((bf16[256,3072]{1,0:T(8,128)(2,1)S(1)}, bf16[256,3072]{1,0:T(8,128)(2,1)S(1)}, u32[]{:S(2)}, u32[]{:S(2)}) %collective-permute-start.7) | collective-permute-done | bytes 1572896 | tf_op jit(solution)/shard_map/ppermute | solution.py:196
  559.6 74.8 %shard_map.137 = bf16[512,3072]{1,0:T(8,128)(2,1)} custom-call(bf16[512,3072]{1,0:T(8,128)(2,1)} %maximum_select_fusion.6.x_hbm, f32[1,3072]{1,0:T(1,128)} %get-tuple-element.35.gain_ref, bf16[2,3072,6144]{2,1,0:T(8,128)(2,1)} %wg_hbm.7, bf16[2,3072,6144]{2,1,0:T(8,128)(2,1)} %wu_hbm.7, bf16[2,6144,3072]{2,1,0:T(8,128)(2,1)} %wd_hbm.7), custom_call_target="tpu_custom_call" | custom-call | flops 57982058496 | bytes 119537664 | tf_op jit(solution)/shard_map/pallas_call | solution.py:164
  641.2 74.8 %shard_map.133 = bf16[512,3072]{1,0:T(8,128)(2,1)} custom-call(bf16[512,3072]{1,0:T(8,128)(2,1)} %maximum_select_fusion.2.x_hbm, f32[1,3072]{1,0:T(1,128)} %get-tuple-element.35.gain_ref, bf16[2,3072,6144]{2,1,0:T(8,128)(2,1)} %wg_hbm.7, bf16[2,3072,6144]{2,1,0:T(8,128)(2,1)} %wu_hbm.7, bf16[2,6144,3072]{2,1,0:T(8,128)(2,1)} %wd_hbm.7), custom_call_target="tpu_custom_call" | custom-call | flops 57982058496 | bytes 119537664 | tf_op jit(solution)/shard_map/pallas_call | solution.py:164
  723.5 32.8 %collective-permute-done.22 = bf16[256,3072]{1,0:T(8,128)(2,1)S(1)} collective-permute-done((bf16[256,3072]{1,0:T(8,128)(2,1)S(1)}, bf16[256,3072]{1,0:T(8,128)(2,1)S(1)}, u32[]{:S(2)}, u32[]{:S(2)}) %collective-permute-start.22) | collective-permute-done | bytes 1572896 | tf_op jit(solution)/shard_map/ppermute | solution.py:196
  757.1 31.9 %collective-permute-done.10 = bf16[256,3072]{1,0:T(8,128)(2,1)S(1)} collective-permute-done((bf16[256,3072]{1,0:T(8,128)(2,1)S(1)}, bf16[256,3072]{1,0:T(8,128)(2,1)S(1)}, u32[]{:S(2)}, u32[]{:S(2)}) %collective-permute-start.10) | collective-permute-done | bytes 1572896 | tf_op jit(solution)/shard_map/ppermute | solution.py:196
  (205 shorter events, 116.7 us)
Async XLA Ops:
  67.1 36.3 %collective-permute-start = (bf16[256,3072]{1,0:T(8,128)(2,1)}, bf16[256,3072]{1,0:T(8,128)(2,1)}, u32[]{:S(2)}, u32[]{:S(2)}) collective-permute-start(bf16[256,3072]{1,0:T(8,128)(2,1)} %constant_dynamic-slice_fusion.7), channel_id=1, source_target_pairs={{0,1},{1,0},{2,3},{3,2},{4,5},{5,4},{6,7},{7,6}} | collective-permute-start | bytes 4718600 | tf_op jit(solution)/shard_map/ppermute | solution.py:194
  102.6 6.6 collective-permute-start.12
  105.9 38.5 %collective-permute-start.1 = (bf16[256,3072]{1,0:T(8,128)(2,1)S(1)}, bf16[256,3072]{1,0:T(8,128)(2,1)S(1)}, u32[]{:S(2)}, u32[]{:S(2)}) collective-permute-start(bf16[256,3072]{1,0:T(8,128)(2,1)S(1)} %add_convert_fusion.13), channel_id=1, source_target_pairs={{0,2},{1,3},{2,0},{3,1},{4,6},{5,7},{6,4},{7,5}} | collective-permute-start | bytes 4718600 | tf_op jit(solution)/shard_map/ppermute | solution.py:196
  112.3 65.2 %collective-permute-start.13 = (bf16[256,3072]{1,0:T(8,128)(2,1)}, bf16[256,3072]{1,0:T(8,128)(2,1)}, u32[]{:S(2)}, u32[]{:S(2)}) collective-permute-start(bf16[256,3072]{1,0:T(8,128)(2,1)} %add_convert_fusion.6), channel_id=1, source_target_pairs={{0,2},{1,3},{2,0},{3,1},{4,6},{5,7},{6,4},{7,5}} | collective-permute-start | bytes 4718600 | tf_op jit(solution)/shard_map/ppermute | solution.py:196
  146.4 34.9 %collective-permute-start.2 = (bf16[256,3072]{1,0:T(8,128)(2,1)}, bf16[256,3072]{1,0:T(8,128)(2,1)}, u32[]{:S(2)}, u32[]{:S(2)}) collective-permute-start(bf16[256,3072]{1,0:T(8,128)(2,1)} %fusion.29), channel_id=1, source_target_pairs={{0,1},{1,0},{2,3},{3,2},{4,5},{5,4},{6,7},{7,6}} | collective-permute-start | bytes 4718600 | tf_op jit(solution)/shard_map/ppermute | solution.py:199
  181.3 82.3 %collective-permute-start.14 = (bf16[256,3072]{1,0:T(8,128)(2,1)}, bf16[256,3072]{1,0:T(8,128)(2,1)S(1)}, u32[]{:S(2)}, u32[]{:S(2)}) collective-permute-start(bf16[256,3072]{1,0:T(8,128)(2,1)} %fusion.28), channel_id=1, source_target_pairs={{0,1},{1,0},{2,3},{3,2},{4,5},{5,4},{6,7},{7,6}} | collective-permute-start | bytes 4718600 | tf_op jit(solution)/shard_map/ppermute | solution.py:199
  263.1 80.5 %collective-permute-start.3 = (bf16[256,3072]{1,0:T(8,128)(2,1)}, bf16[256,3072]{1,0:T(8,128)(2,1)S(1)}, u32[]{:S(2)}, u32[]{:S(2)}) collective-permute-start(bf16[256,3072]{1,0:T(8,128)(2,1)} %constant_dynamic-slice_fusion.6), channel_id=1, source_target_pairs={{0,1},{1,0},{2,3},{3,2},{4,5},{5,4},{6,7},{7,6}} | collective-permute-start | bytes 4718600 | tf_op jit(solution)/shard_map/ppermute | solution.py:194
  343.5 3.4 collective-permute-start.15
  344.8 37.3 %copy-start.2 = (bf16[512,3072]{1,0:T(8,128)(2,1)S(1)}, bf16[512,3072]{1,0:T(8,128)(2,1)}, u32[]{:S(2)}) copy-start(bf16[512,3072]{1,0:T(8,128)(2,1)} %maximum_select_fusion.x_hbm) | copy-start | bytes 9437188
  344.8 37.3 %collective-permute-start.4 = (bf16[256,3072]{1,0:T(8,128)(2,1)S(1)}, bf16[256,3072]{1,0:T(8,128)(2,1)S(1)}, u32[]{:S(2)}, u32[]{:S(2)}) collective-permute-start(bf16[256,3072]{1,0:T(8,128)(2,1)S(1)} %add_convert_fusion.12), channel_id=1, source_target_pairs={{0,2},{1,3},{2,0},{3,1},{4,6},{5,7},{6,4},{7,5}} | collective-permute-start | bytes 4718600 | tf_op jit(solution)/shard_map/ppermute | solution.py:196
  347.5 67.3 %copy-start.3 = (bf16[512,3072]{1,0:T(8,128)(2,1)S(1)}, bf16[512,3072]{1,0:T(8,128)(2,1)}, u32[]{:S(2)}) copy-start(bf16[512,3072]{1,0:T(8,128)(2,1)} %maximum_select_fusion.4.x_hbm) | copy-start | bytes 9437188
  347.5 67.3 %collective-permute-start.16 = (bf16[256,3072]{1,0:T(8,128)(2,1)S(1)}, bf16[256,3072]{1,0:T(8,128)(2,1)S(1)}, u32[]{:S(2)}, u32[]{:S(2)}) collective-permute-start(bf16[256,3072]{1,0:T(8,128)(2,1)S(1)} %add_convert_fusion.5), channel_id=1, source_target_pairs={{0,2},{1,3},{2,0},{3,1},{4,6},{5,7},{6,4},{7,5}} | collective-permute-start | bytes 4718600 | tf_op jit(solution)/shard_map/ppermute | solution.py:196
  382.1 34.9 %slice-start.15 = ((s8[6291456]{0:T(1024)(128)(4,1)}), s8[4194304]{0:T(1024)(128)(4,1)S(1)}, s32[]{:S(2)}) async-start(s8[6291456]{0:T(1024)(128)(4,1)} %bitcast.140), calls=%async_computation.15 | async-start | bytes 8388608
  382.9 34.1 %slice-start.16 = ((s8[6291456]{0:T(1024)(128)(4,1)}), s8[2097152]{0:T(1024)(128)(4,1)S(1)}, s32[]{:S(2)}) async-start(s8[6291456]{0:T(1024)(128)(4,1)} %bitcast.140), calls=%async_computation.16 | async-start | bytes 4194304
  382.9 32.8 %collective-permute-start.5 = (bf16[256,3072]{1,0:T(8,128)(2,1)S(1)}, bf16[256,3072]{1,0:T(8,128)(2,1)S(1)}, u32[]{:S(2)}, u32[]{:S(2)}) collective-permute-start(bf16[256,3072]{1,0:T(8,128)(2,1)S(1)} %add_convert_fusion.11), channel_id=1, source_target_pairs={{0,1},{1,0},{2,3},{3,2},{4,5},{5,4},{6,7},{7,6}} | collective-permute-start | bytes 4718600 | tf_op jit(solution)/shard_map/ppermute | solution.py:199
  415.6 10.6 %collective-permute-start.17 = (bf16[256,3072]{1,0:T(8,128)(2,1)S(1)}, bf16[256,3072]{1,0:T(8,128)(2,1)S(1)}, u32[]{:S(2)}, u32[]{:S(2)}) collective-permute-start(bf16[256,3072]{1,0:T(8,128)(2,1)S(1)} %add_convert_fusion.4), channel_id=1, source_target_pairs={{0,1},{1,0},{2,3},{3,2},{4,5},{5,4},{6,7},{7,6}} | collective-permute-start | bytes 4718600 | tf_op jit(solution)/shard_map/ppermute | solution.py:199
  459.1 22.0 %collective-permute-start.18 = (bf16[256,3072]{1,0:T(8,128)(2,1)}, bf16[256,3072]{1,0:T(8,128)(2,1)}, u32[]{:S(2)}, u32[]{:S(2)}) collective-permute-start(bf16[256,3072]{1,0:T(8,128)(2,1)} %constant_dynamic-slice_fusion.1), channel_id=1, source_target_pairs={{0,1},{1,0},{2,3},{3,2},{4,5},{5,4},{6,7},{7,6}} | collective-permute-start | bytes 4718600 | tf_op jit(solution)/shard_map/ppermute | solution.py:194
  481.1 5.5 collective-permute-start.6
  484.8 37.3 %copy-start.9 = (bf16[512,3072]{1,0:T(8,128)(2,1)S(1)}, bf16[512,3072]{1,0:T(8,128)(2,1)}, u32[]{:S(2)}) copy-start(bf16[512,3072]{1,0:T(8,128)(2,1)} %copy-done.8) | copy-start | bytes 9437188
  484.8 37.3 %collective-permute-start.19 = (bf16[256,3072]{1,0:T(8,128)(2,1)S(1)}, bf16[256,3072]{1,0:T(8,128)(2,1)S(1)}, u32[]{:S(2)}, u32[]{:S(2)}) collective-permute-start(bf16[256,3072]{1,0:T(8,128)(2,1)S(1)} %add_convert_fusion.3), channel_id=1, source_target_pairs={{0,2},{1,3},{2,0},{3,1},{4,6},{5,7},{6,4},{7,5}} | collective-permute-start | bytes 4718600 | tf_op jit(solution)/shard_map/ppermute | solution.py:196
  487.2 67.7 %collective-permute-start.7 = (bf16[256,3072]{1,0:T(8,128)(2,1)S(1)}, bf16[256,3072]{1,0:T(8,128)(2,1)S(1)}, u32[]{:S(2)}, u32[]{:S(2)}) collective-permute-start(bf16[256,3072]{1,0:T(8,128)(2,1)S(1)} %add_convert_fusion.10), channel_id=1, source_target_pairs={{0,2},{1,3},{2,0},{3,1},{4,6},{5,7},{6,4},{7,5}} | collective-permute-start | bytes 4718600 | tf_op jit(solution)/shard_map/ppermute | solution.py:196
  522.9 33.9 %collective-permute-start.20 = (bf16[256,3072]{1,0:T(8,128)(2,1)S(1)}, bf16[256,3072]{1,0:T(8,128)(2,1)S(1)}, u32[]{:S(2)}, u32[]{:S(2)}) collective-permute-start(bf16[256,3072]{1,0:T(8,128)(2,1)S(1)} %add_convert_fusion.2), channel_id=1, source_target_pairs={{0,1},{1,0},{2,3},{3,2},{4,5},{5,4},{6,7},{7,6}} | collective-permute-start | bytes 4718600 | tf_op jit(solution)/shard_map/ppermute | solution.py:199
  556.8 80.6 %collective-permute-start.8 = (bf16[256,3072]{1,0:T(8,128)(2,1)}, bf16[256,3072]{1,0:T(8,128)(2,1)S(1)}, u32[]{:S(2)}, u32[]{:S(2)}) collective-permute-start(bf16[256,3072]{1,0:T(8,128)(2,1)} %add_convert_fusion.9), channel_id=1, source_target_pairs={{0,1},{1,0},{2,3},{3,2},{4,5},{5,4},{6,7},{7,6}} | collective-permute-start | bytes 4718600 | tf_op jit(solution)/shard_map/ppermute | solution.py:199
  637.0 80.7 %collective-permute-start.21 = (bf16[256,3072]{1,0:T(8,128)(2,1)}, bf16[256,3072]{1,0:T(8,128)(2,1)S(1)}, u32[]{:S(2)}, u32[]{:S(2)}) collective-permute-start(bf16[256,3072]{1,0:T(8,128)(2,1)} %constant_dynamic-slice_fusion), channel_id=1, source_target_pairs={{0,1},{1,0},{2,3},{3,2},{4,5},{5,4},{6,7},{7,6}} | collective-permute-start | bytes 4718600 | tf_op jit(solution)/shard_map/ppermute | solution.py:194
  717.6 3.4 collective-permute-start.9
  718.9 37.3 %copy-start = (bf16[512,3072]{1,0:T(8,128)(2,1)S(1)}, bf16[512,3072]{1,0:T(8,128)(2,1)}, u32[]{:S(2)}) copy-start(bf16[512,3072]{1,0:T(8,128)(2,1)} %maximum_select_fusion.6.x_hbm) | copy-start | bytes 9437188
  718.9 37.3 %collective-permute-start.22 = (bf16[256,3072]{1,0:T(8,128)(2,1)S(1)}, bf16[256,3072]{1,0:T(8,128)(2,1)S(1)}, u32[]{:S(2)}, u32[]{:S(2)}) collective-permute-start(bf16[256,3072]{1,0:T(8,128)(2,1)S(1)} %add_convert_fusion.1), channel_id=1, source_target_pairs={{0,2},{1,3},{2,0},{3,1},{4,6},{5,7},{6,4},{7,5}} | collective-permute-start | bytes 4718600 | tf_op jit(solution)/shard_map/ppermute | solution.py:196
  721.7 67.3 %copy-start.1 = (bf16[512,3072]{1,0:T(8,128)(2,1)S(1)}, bf16[512,3072]{1,0:T(8,128)(2,1)}, u32[]{:S(2)}) copy-start(bf16[512,3072]{1,0:T(8,128)(2,1)} %maximum_select_fusion.2.x_hbm) | copy-start | bytes 9437188
  721.7 67.3 %collective-permute-start.10 = (bf16[256,3072]{1,0:T(8,128)(2,1)S(1)}, bf16[256,3072]{1,0:T(8,128)(2,1)S(1)}, u32[]{:S(2)}, u32[]{:S(2)}) collective-permute-start(bf16[256,3072]{1,0:T(8,128)(2,1)S(1)} %add_convert_fusion.8), channel_id=1, source_target_pairs={{0,2},{1,3},{2,0},{3,1},{4,6},{5,7},{6,4},{7,5}} | collective-permute-start | bytes 4718600 | tf_op jit(solution)/shard_map/ppermute | solution.py:196
  757.0 32.8 %copy-start.23 = (bf16[4,512,256]{2,1,0:T(8,128)(2,1)S(1)}, bf16[4,512,256]{2,1,0:T(8,128)(2,1)}, u32[]{:S(2)}) copy-start(bf16[4,512,256]{2,1,0:T(8,128)(2,1)} %get-tuple-element.15) | copy-start | bytes 3145732
  757.1 38.8 %collective-permute-start.23 = (bf16[256,3072]{1,0:T(8,128)(2,1)S(1)}, bf16[256,3072]{1,0:T(8,128)(2,1)S(1)}, u32[]{:S(2)}, u32[]{:S(2)}) collective-permute-start(bf16[256,3072]{1,0:T(8,128)(2,1)S(1)} %add_convert_fusion), channel_id=1, source_target_pairs={{0,1},{1,0},{2,3},{3,2},{4,5},{5,4},{6,7},{7,6}} | collective-permute-start | bytes 4718600 | tf_op jit(solution)/shard_map/ppermute | solution.py:199
  789.8 7.4 collective-permute-start.11
  (45 other events, 377.5 us)

commit v3 on v0

v3 whole, which is shorter than its diff:
```python
import jax
import jax.numpy as jnp
from jax import lax
from jax.experimental import pallas as pl
from jax.experimental.pallas import tpu as pltpu
from jax.sharding import PartitionSpec as P

RMS_EPS = 1e-6
ROPE_BASE = 10000.0
TILE = 512
NORM_ROWS = 64
F32, BF16 = jnp.float32, jnp.bfloat16


def rope_tables(seq_len, head_dim):
    half_dim = head_dim // 2
    inv_freq = ROPE_BASE ** (-jnp.arange(half_dim, dtype=F32) * (2.0 / head_dim))
    angles = jnp.arange(seq_len, dtype=F32)[:, None] * inv_freq[None, :]
    return jnp.cos(angles), jnp.sin(angles)


def block(i, size):
    return pl.ds(pl.multiple_of(i * size, size), size)


def kernel(
    len_ref, hidden, w_query, w_key, w_value, w_out, w_gate, w_up, w_down, gain_attn, gain_mlp, cos_ref, sin_ref,
    h_out, k_cache, v_cache,
    x, a, m, wa, wb, raw, ga, ub, part, recv1, recv2,
    x_sem, wa_sem, wb_sem, raw_sem, wo_sem, kc_sem, vc_sem, s1, r1, s2, r2, s3, r3,
):
    n_layers, model, heads, dim = w_query.shape
    prompts, seq, _ = hidden.shape
    inner = heads * dim
    n_gu = w_gate.shape[2] // TILE
    n_down = model // TILE
    half = seq // 2
    n_raw = raw_sem.shape[0]
    raw_rows = model // n_raw
    half_dim = dim // 2

    me = lax.axis_index("tp")
    core = lax.rem(me, 2)
    peer = {"tp": me + 1 - 2 * core}
    far = {"tp": lax.rem(me + 2, 4)}
    own = block(core, half)
    other = block(1 - core, half)

    def remote(src, dst, send_sem, recv_sem, device):
        return pltpu.make_async_remote_copy(src, dst, send_sem, recv_sem, device_id=device, device_id_type=pl.DeviceIdType.MESH)

    def send_part(b, t):
        c = block(t, TILE)
        return remote(part.at[b, other, c], recv1.at[b, :, c], s1.at[b, t], r1.at[b, t], peer)

    def send_far(b, stage, t):
        c = block(t, TILE)
        return remote(part.at[b, own, c], recv2.at[stage, b, :, c], s2.at[b, t], r2.at[stage, b, t], far)

    def send_x(b, t):
        c = block(t, TILE)
        return remote(x.at[b, own, c], x.at[b, own, c], s3.at[b, t], r3.at[b, t], peer)

    def chip_add(b, stage, t):
        c = block(t, TILE)
        send_part(b, t).wait_recv()
        part[b, own, c] = (part[b, own, c].astype(F32) + recv1[b, :, c].astype(F32)).astype(BF16)
        send_far(b, stage, t).start()

    def finish_sum(b, stage):
        def body(t, _):
            c = block(t, TILE)
            send_far(b, stage, t).wait_recv()
            total = part[b, own, c].astype(F32) + recv2[stage, b, :, c].astype(F32)
            x[b, own, c] = (x[b, own, c].astype(F32) + total).astype(BF16)
            send_x(b, t).start()
            return 0

        lax.fori_loop(0, n_down, body, 0)

    def finish_wait(b, stage):
        def body(t, _):
            send_part(b, t).wait_send()
            send_far(b, stage, t).wait_send()
            send_x(b, t).wait()
            return 0

        lax.fori_loop(0, n_down, body, 0)

    def norm(b, gain_ref, layer):
        gain = 1.0 + gain_ref[pl.ds(layer, 1), :]

        def body(i, _):
            rows = block(i, NORM_ROWS)
            v = x[b, rows, :].astype(F32)
            mean_sq = jnp.mean(v * v, axis=-1, keepdims=True)
            a[rows, :] = (v * lax.rsqrt(mean_sq + RMS_EPS) * gain).astype(BF16)
            return 0

        lax.fori_loop(0, seq // NORM_ROWS, body, 0)

    def raw_copy(w, layer, c):
        rows = pl.ds(c * raw_rows, raw_rows)
        return pltpu.make_async_copy(w.at[layer, rows], raw.at[rows], raw_sem.at[c])

    def raw_start(w, layer):
        for c in range(n_raw):
            raw_copy(w, layer, c).start()

    def raw_wait(w, layer):
        for c in range(n_raw):
            raw_copy(w, layer, c).wait()

    def relayout(slot):
        for c in range(n_raw):
            rows = pl.ds(c * raw_rows, raw_rows)
            v = raw[rows].reshape(raw_rows, inner)
            wa[slot, rows, :] = v[:, :TILE]
            wb[slot, rows, :] = v[:, TILE:]

    def out_copy(layer, t):
        dst = (wa if t < 3 else wb).at[1, pl.ds((t % 3) * inner, inner), :]
        return pltpu.make_async_copy(w_out.at[layer, :, pl.ds(t * TILE, TILE)], dst, wo_sem.at[t])

    def gu_copies(layer, t, slot):
        c = block(t, TILE)
        return (
            pltpu.make_async_copy(w_gate.at[layer, :, c], wa.at[slot], wa_sem.at[slot]),
            pltpu.make_async_copy(w_up.at[layer, :, c], wb.at[slot], wb_sem.at[slot]),
        )

    def down_copies(layer, t, slot):
        c = block(t, TILE)
        return (
            pltpu.make_async_copy(w_down.at[layer, pl.ds(0, model), c], wa.at[slot], wa_sem.at[slot]),
            pltpu.make_async_copy(w_down.at[layer, pl.ds(model, model), c], wb.at[slot], wb_sem.at[slot]),
        )

    def start(copies):
        for c in copies:
            c.start()

    def wait(copies):
        for c in copies:
            c.wait()

    def dot(p, q):
        return jnp.dot(p, q, preferred_element_type=F32)

    def cache_copies(layer, b, h):
        return (
            pltpu.make_async_copy(m.at[:, block(heads + h, dim)], k_cache.at[layer, b, h], kc_sem.at[h]),
            pltpu.make_async_copy(m.at[:, block(h, dim)], v_cache.at[layer, b, h], vc_sem.at[h]),
        )

    def head(b, i, j):
        h = 2 * i + j
        lanes = slice(j * dim, (j + 1) * dim)
        cos_t, sin_t = cos_ref[...], sin_ref[...]

        def rope(v):
            lo, hi = v[:, :half_dim], v[:, half_dim:]
            return jnp.concatenate([lo * cos_t - hi * sin_t, hi * cos_t + lo * sin_t], axis=-1)

        q = (rope(ga[i, :, lanes]) * (dim ** -0.5)).astype(BF16)
        k = rope(ub[i, :, lanes]).astype(BF16)
        m[:, block(heads + h, dim)] = k
        for r in range(2):
            keys = (r + 1) * half
            v = m[pl.ds(0, keys), block(h, dim)]
            scores = lax.dot_general(q[r * half:keys], k[:keys], (((1,), (1,)), ((), ())), preferred_element_type=F32)
            row = r * half + lax.broadcasted_iota(jnp.int32, (half, keys), 0)
            col = lax.broadcasted_iota(jnp.int32, (half, keys), 1)
            scores = jnp.where((col <= row) & (col < len_ref[b]), scores, -1e30)
            p = jnp.exp(scores - jnp.max(scores, axis=-1, keepdims=True))
            p = (p * (1.0 / jnp.sum(p, axis=-1, keepdims=True))).astype(BF16)
            m[pl.ds(r * half, half), block(2 * heads + h, dim)] = dot(p, v).astype(BF16)

    def attn_phase(layer, b):
        norm(b, gain_attn, layer)
        raw_wait(w_query, layer)
        relayout(0)
        raw_start(w_key, layer)
        ga[0] = dot(a[...], wa[0])
        raw_wait(w_key, layer)
        relayout(1)
        ga[1] = dot(a[...], wb[0])
        raw_start(w_value, layer)
        ub[0] = dot(a[...], wa[1])
        raw_wait(w_value, layer)
        relayout(0)
        ub[1] = dot(a[...], wb[1])
        for t in range(n_down):
            out_copy(layer, t).start()

        @pl.when(b == 0)
        def _():
            raw_start(w_query, layer)

        m[:, pl.ds(0, TILE)] = dot(a[...], wa[0]).astype(BF16)
        m[:, pl.ds(TILE, TILE)] = dot(a[...], wb[0]).astype(BF16)

        @pl.when(b == 1)
        def _():
            start(gu_copies(layer, 0, 0))

        def two_heads(i, _):
            head(b, i, 0)
            head(b, i, 1)
            start(cache_copies(layer, b, 2 * i))
            start(cache_copies(layer, b, 2 * i + 1))
            return 0

        lax.fori_loop(0, heads // 2, two_heads, 0)

        @pl.when((b == 0) & (layer > 0))
        def _():
            finish_sum(1, 1)

        for t in range(n_down):
            out_copy(layer, t).wait()
        o_cols = pl.ds(2 * inner, inner)

        def project(i, _):
            @pl.when(i > 0)
            def _():
                send_part(b, i - 1).start()
                send_part(b, i + 2).start()

            part[b, :, block(i, TILE)] = dot(m[:, o_cols], wa[1, block(i, inner), :]).astype(BF16)
            part[b, :, block(i + 3, TILE)] = dot(m[:, o_cols], wb[1, block(i, inner), :]).astype(BF16)
            return 0

        lax.fori_loop(0, 3, project, 0)
        for h in range(heads):
            wait(cache_copies(layer, b, h))
        send_part(b, 2).start()
        send_part(b, 5).start()
        for t in (0, 3, 1, 4, 2, 5):
            chip_add(b, 0, t)

        @pl.when((b == 0) & (layer > 0))
        def _():
            finish_wait(1, 1)

        @pl.when(b == 1)
        def _():
            finish_sum(0, 0)
            finish_wait(0, 0)

    def mlp_phase(layer, b):
        @pl.when((b == 1) & (layer + 1 < n_layers))
        def _():
            raw_start(w_query, layer + 1)

        norm(b, gain_mlp, layer)

        def activate(t, slot):
            m[:, block(t, TILE)] = (jax.nn.gelu(ga[slot], approximate=True) * ub[slot]).astype(BF16)

        def gate_up(t, slot):
            wait(gu_copies(layer, t, slot))

            @pl.when(t + 1 < n_gu)
            def _():
                start(gu_copies(layer, t + 1, 1 - slot))

            @pl.when(t + 1 == n_gu)
            def _():
                start(down_copies(layer, 0, 1 - slot))

            activate(lax.rem(t + n_gu - 1, n_gu), 1 - slot)
            ga[slot] = dot(a[...], wa[slot])
            ub[slot] = dot(a[...], wb[slot])

        def gate_up_pair(i, _):
            gate_up(2 * i, 0)
            gate_up(2 * i + 1, 1)
            return 0

        lax.fori_loop(0, n_gu // 2, gate_up_pair, 0)
        activate(n_gu - 1, 1)
        finish_sum(1 - b, b)

        def down(t, slot):
            wait(down_copies(layer, t, slot))

            @pl.when(t + 1 < n_down)
            def _():
                start(down_copies(layer, t + 1, 1 - slot))

            @pl.when((t + 1 == n_down) & (b == 0))
            def _():
                start(gu_copies(layer, 0, 1 - slot))

            @pl.when(t > 0)
            def _():
                send_part(b, t - 1).start()

            @pl.when(t > 1)
            def _():
                chip_add(b, 1, t - 2)

            part[b, :, block(t, TILE)] = (
                dot(m[:, pl.ds(0, model)], wa[slot]) + dot(m[:, pl.ds(model, model)], wb[slot])
            ).astype(BF16)

        def down_pair(i, _):
            down(2 * i, 0)
            down(2 * i + 1, 1)
            return 0

        lax.fori_loop(0, n_down // 2, down_pair, 0)
        finish_wait(1 - b, b)
        send_part(b, n_down - 1).start()
        chip_add(b, 1, n_down - 2)
        chip_add(b, 1, n_down - 1)

    hidden_copies = [pltpu.make_async_copy(hidden.at[b], x.at[b], x_sem.at[b]) for b in range(prompts)]
    start(hidden_copies)
    raw_start(w_query, 0)
    barrier = pltpu.get_barrier_semaphore()
    for device in (peer, far):
        pl.semaphore_signal(barrier, inc=1, device_id=device, device_id_type=pl.DeviceIdType.MESH)
    wait(hidden_copies)
    pl.semaphore_wait(barrier, 2)

    def layer_step(layer, _):
        def attn_step(b, _):
            attn_phase(layer, b)
            return 0

        def mlp_step(b, _):
            mlp_phase(layer, b)
            return 0

        lax.fori_loop(0, prompts, attn_step, 0)
        lax.fori_loop(0, prompts, mlp_step, 0)
        return 0

    lax.fori_loop(0, n_layers, layer_step, 0)
    out_copies = [pltpu.make_async_copy(x.at[b], h_out.at[b], x_sem.at[b]) for b in range(prompts)]
    out_copies[0].start()
    finish_sum(1, 1)
    finish_wait(1, 1)
    out_copies[1].start()
    wait(out_copies)


def solution(mesh):
    head_cols = P(None, None, "tp", None)
    head_rows = P(None, "tp", None, None)
    ff_cols = P(None, None, "tp")
    ff_rows = P(None, "tp", None)

    def shard_body(hidden, lengths, w_query, w_key, w_value, w_out, w_gate, w_up, w_down, norm_attn, norm_mlp):
        n_layers, model, heads, dim = w_query.shape
        prompts, seq, _ = hidden.shape
        width = w_gate.shape[2]
        inner = heads * dim
        n_down = model // TILE
        half = seq // 2
        cos_t, sin_t = rope_tables(seq, dim)
        anywhere = pl.BlockSpec(memory_space=pl.ANY)
        vmem = pl.BlockSpec(memory_space=pltpu.VMEM)
        dma = pltpu.SemaphoreType.DMA
        cache = jax.ShapeDtypeStruct((n_layers, prompts, heads, seq, dim), BF16)
        return pl.pallas_call(
            kernel,
            in_specs=[pl.BlockSpec(memory_space=pltpu.SMEM)] + [anywhere] * 8 + [vmem] * 4,
            out_specs=[anywhere] * 3,
            out_shape=[jax.ShapeDtypeStruct(hidden.shape, BF16), cache, cache],
            scratch_shapes=[
                pltpu.VMEM((prompts, seq, model), BF16),
                pltpu.VMEM((seq, model), BF16),
                pltpu.VMEM((seq, width), BF16),
                pltpu.VMEM((2, model, TILE), BF16),
                pltpu.VMEM((2, model, TILE), BF16),
                pltpu.VMEM((model, heads, dim), BF16),
                pltpu.VMEM((2, seq, TILE), F32),
                pltpu.VMEM((2, seq, TILE), F32),
                pltpu.VMEM((prompts, seq, model), BF16),
                pltpu.VMEM((prompts, half, model), BF16),
                pltpu.VMEM((2, prompts, half, model), BF16),
                dma((prompts,)), dma((2,)), dma((2,)), dma((4,)), dma((n_down,)), dma((heads,)), dma((heads,)),
                dma((prompts, n_down)), dma((prompts, n_down)), dma((prompts, n_down)), dma((2, prompts, n_down)),
                dma((prompts, n_down)), dma((prompts, n_down)),
            ],
            compiler_params=pltpu.CompilerParams(
                collective_id=0, has_side_effects=True, vmem_limit_bytes=63 * 1024 * 1024
            ),
        )(
            lengths, hidden, w_query, w_key, w_value, w_out.reshape(n_layers, inner, model), w_gate, w_up, w_down,
            norm_attn, norm_mlp, cos_t, sin_t,
        )

    return jax.shard_map(
        shard_body,
        mesh=mesh,
        in_specs=(P("dp"), P("dp"), head_cols, head_cols, head_cols, head_rows, ff_cols, ff_cols, ff_rows, P(), P()),
        out_specs=(P("dp"), P(None, "dp", "tp"), P(None, "dp", "tp")),
        check_vma=False,
    )
```

time: 972 us -> 468 us (0.48)
  Pallas kernels: 0 us -> 455 us
  waiting for transfers between devices: 420 us -> 0 us
  matrix products: 377 us -> 0 us
  local copies, waits for them, and re-layouts: 85.1 us -> 10.5 us
  other arithmetic: 72.7 us -> 1.75 us
  between operations: 14.5 us -> 0.66 us
    pallas_call x0 -> x1, Pallas kernels: none -> 455 us  [shard_body(): pl.pallas_call(kernel, in_specs=[pl.BlockSpec(memory_space=pltpu.SMEM)] +...]
    psum x4 -> x0, waiting for transfers between devices: 419 us -> none  [shard_body(): summed = lax.psum(part_sum, 'tp')]
    dot_general x16 -> x0, matrix products: 377 us -> none  [the longest x2 100 us: mlp_partial(): jnp.einsum('bsm,mf->bsf', normed, w_up, preferred_element_type=jnp.float32)]
    unnamed x69 -> x7, local copies, waits for them, and re-layouts: 55.2 us -> 10.5 us
    reduce_sum x4 -> x0, other arithmetic: 35 us -> none  [rms_norm(): mean_sq = jnp.mean(x_f32 * x_f32, axis=-1, keepdims=True)]
    slice x3 -> x0, local copies, waits for them, and re-layouts: 29.9 us -> none  [the longest x1 12.2 us: shard_body(): w_query[layer_idx]]
    another operation x5 -> x0, other arithmetic: 13.1 us -> none  [the longest x3 7.99 us: shard_body(): return (hidden_state, jnp.stack(key_list), jnp.stack(value_list))]
    sub x2 -> x0, other arithmetic: 11 us -> none  [attention(): attn_probs = jax.nn.softmax(scores, axis=-1).astype(jnp.bfloat16)]
  transfers between devices with their start and end apart: 4 -> 0, of which waited for: 4 -> 0; matrix products, arithmetic and copies ran while one was open for 4% -> 0% of each run, Pallas kernels for 0% -> 0%
where the time goes in v3:
time: 468 us
  Pallas kernels  455 us (97%)
  local copies, waits for them, and re-layouts  10.5 us (2%)
    pallas_call x1, Pallas kernels, shard_body(): pl.pallas_call(kernel, in_specs=[pl.BlockSpec(memory_space=pltpu.SMEM)] +...  455 us
    unnamed x7, local copies, waits for them, and re-layouts  10.5 us

profile of v3, /device:TPU:0, one launch (start us, length us, event | category | flops | bytes accessed | tf_op | source)
XLA Modules:
  0.0 467.9 jit_solution(14988012722028499495)
XLA Ops:
  0.6 1.7 fusion
  2.4 455.0 %shard_map.130 = (bf16[2,512,3072]{2,1,0:T(8,128)(2,1)}, bf16[2,2,4,512,256]{4,3,2,1,0:T(8,128)(2,1)}, bf16[2,2,4,512,256]{4,3,2,1,0:T(8,128)(2,1)}) custom-call(s32[2]{0:T(128)} %len_ref.1, bf16[2,512,3072]{2,1,0:T(8,128)(2,1)} %hidden.1, bf16[2,3072,4,256]{3,2,1,0:T(4,128)(2,1)} %w_query.1, bf16[2,3072,4,256]{3,2,1,0:T(4,128)(2,1)} %w_key.1, ...), custom_call_target="tpu_custom_call" | custom-call | tf_op jit(solution)/shard_map/pallas_call | solution.py:368
  457.3 0.0 copy-start.1
  457.4 0.0 copy-start
  457.4 6.5 %copy.17 = bf16[2,512,3072]{2,1,0:T(8,128)(2,1)} copy(bf16[2,512,3072]{2,1,0:T(8,128)(2,1)} %get-tuple-element.8) | data formatting | bytes 12582912
  463.9 0.0 copy-done.1
  463.9 2.0 copy.18
  465.9 0.0 copy-done
  465.9 2.0 copy.19
  (1 shorter events, 0.0 us)
Async XLA Ops:
  457.3 6.5 %copy-start.1 = (bf16[2,2,4,512,256]{4,3,2,1,0:T(8,128)(2,1)S(1)}, bf16[2,2,4,512,256]{4,3,2,1,0:T(8,128)(2,1)}, u32[]{:S(2)}) copy-start(bf16[2,2,4,512,256]{4,3,2,1,0:T(8,128)(2,1)} %get-tuple-element.9) | copy-start | bytes 12582916
  457.4 8.5 %copy-start = (bf16[2,2,4,512,256]{4,3,2,1,0:T(8,128)(2,1)S(1)}, bf16[2,2,4,512,256]{4,3,2,1,0:T(8,128)(2,1)}, u32[]{:S(2)}) copy-start(bf16[2,2,4,512,256]{4,3,2,1,0:T(8,128)(2,1)} %get-tuple-element.10) | copy-start | bytes 12582916

commit v4 on v3

--- a/solution.py
+++ b/solution.py
@@ -1,5 +1,6 @@
 import jax
 import jax.numpy as jnp
+import numpy as np
 from jax import lax
 from jax.experimental import pallas as pl
 from jax.experimental.pallas import tpu as pltpu
@@ -9,14 +10,16 @@
 ROPE_BASE = 10000.0
 TILE = 512
 NORM_ROWS = 64
+ACT_ROWS = 16
+SPREAD_ROWS = 96
 F32, BF16 = jnp.float32, jnp.bfloat16
 
 
 def rope_tables(seq_len, head_dim):
     half_dim = head_dim // 2
-    inv_freq = ROPE_BASE ** (-jnp.arange(half_dim, dtype=F32) * (2.0 / head_dim))
-    angles = jnp.arange(seq_len, dtype=F32)[:, None] * inv_freq[None, :]
-    return jnp.cos(angles), jnp.sin(angles)
+    inv_freq = np.float32(ROPE_BASE) ** (-np.arange(half_dim, dtype=np.float32) * np.float32(2.0 / head_dim))
+    angles = np.arange(seq_len, dtype=np.float32)[:, None] * inv_freq[None, :].astype(np.float32)
+    return np.cos(angles).astype(np.float32), np.sin(angles).astype(np.float32)
 
 
 def block(i, size):
@@ -24,8 +27,8 @@
 
 
 def kernel(
-    len_ref, hidden, w_query, w_key, w_value, w_out, w_gate, w_up, w_down, gain_attn, gain_mlp, cos_ref, sin_ref,
-    h_out, k_cache, v_cache,
+    len_ref, hidden, w_query, w_key, w_value, w_out, w_gate, w_up, w_down, gains, cos_ref, sin_ref,
+    h_out0, h_out1, k_cache, v_cache,
     x, a, m, wa, wb, raw, ga, ub, part, recv1, recv2,
     x_sem, wa_sem, wb_sem, raw_sem, wo_sem, kc_sem, vc_sem, s1, r1, s2, r2, s3, r3,
 ):
@@ -87,14 +90,14 @@
 
         lax.fori_loop(0, n_down, body, 0)
 
-    def norm(b, gain_ref, layer):
-        gain = 1.0 + gain_ref[pl.ds(layer, 1), :]
-
+    def norm_rows(b, which, rows):
+        v = x[b, rows, :].astype(F32)
+        mean_sq = jnp.mean(v * v, axis=-1, keepdims=True)
+        a[rows, :] = (v * lax.rsqrt(mean_sq + RMS_EPS) * (1.0 + gains[pl.ds(which, 1), :])).astype(BF16)
+
+    def norm(b, which):
         def body(i, _):
-            rows = block(i, NORM_ROWS)
-            v = x[b, rows, :].astype(F32)
-            mean_sq = jnp.mean(v * v, axis=-1, keepdims=True)
-            a[rows, :] = (v * lax.rsqrt(mean_sq + RMS_EPS) * gain).astype(BF16)
+            norm_rows(b, which, block(i, NORM_ROWS))
             return 0
 
         lax.fori_loop(0, seq // NORM_ROWS, body, 0)
@@ -176,29 +179,47 @@
             p = (p * (1.0 / jnp.sum(p, axis=-1, keepdims=True))).astype(BF16)
             m[pl.ds(r * half, half), block(2 * heads + h, dim)] = dot(p, v).astype(BF16)
 
+    hidden_copies = [pltpu.make_async_copy(hidden.at[b], x.at[b], x_sem.at[b]) for b in range(prompts)]
+
     def attn_phase(layer, b):
-        norm(b, gain_attn, layer)
+        @pl.when((layer == 0) & (b == 1))
+        def _():
+            hidden_copies[1].wait()
+
+        @pl.when((layer == 0) | (b == 1))
+        def _():
+            norm(b, 2 * layer)
+
         raw_wait(w_query, layer)
         relayout(0)
         raw_start(w_key, layer)
         ga[0] = dot(a[...], wa[0])
+        ga[1] = dot(a[...], wb[0])
+
+        @pl.when(b == 1)
+        def _():
+            chip_add(0, 0, 2)
+            chip_add(0, 0, 5)
+
+        @pl.when((b == 0) & (layer > 0))
+        def _():
+            chip_add(1, 1, n_down - 1)
+
         raw_wait(w_key, layer)
         relayout(1)
-        ga[1] = dot(a[...], wb[0])
         raw_start(w_value, layer)
         ub[0] = dot(a[...], wa[1])
-        raw_wait(w_value, layer)
-        relayout(0)
         ub[1] = dot(a[...], wb[1])
         for t in range(n_down):
             out_copy(layer, t).start()
-
-        @pl.when(b == 0)
-        def _():
-            raw_start(w_query, layer)
-
+        raw_wait(w_value, layer)
+        relayout(0)
         m[:, pl.ds(0, TILE)] = dot(a[...], wa[0]).astype(BF16)
         m[:, pl.ds(TILE, TILE)] = dot(a[...], wb[0]).astype(BF16)
+
+        @pl.when(b == 0)
+        def _():
+            raw_start(w_query, layer)
 
         @pl.when(b == 1)
         def _():
@@ -236,7 +257,7 @@
             wait(cache_copies(layer, b, h))
         send_part(b, 2).start()
         send_part(b, 5).start()
-        for t in (0, 3, 1, 4, 2, 5):
+        for t in (0, 3, 1, 4):
             chip_add(b, 0, t)
 
         @pl.when((b == 0) & (layer > 0))
@@ -245,6 +266,8 @@
 
         @pl.when(b == 1)
         def _():
+            chip_add(1, 0, 2)
+            chip_add(1, 0, 5)
             finish_sum(0, 0)
             finish_wait(0, 0)
 
@@ -253,10 +276,9 @@
         def _():
             raw_start(w_query, layer + 1)
 
-        norm(b, gain_mlp, layer)
-
-        def activate(t, slot):
-            m[:, block(t, TILE)] = (jax.nn.gelu(ga[slot], approximate=True) * ub[slot]).astype(BF16)
+        @pl.when(b == 0)
+        def _():
+            norm(b, 2 * layer + 1)
 
         def gate_up(t, slot):
             wait(gu_copies(layer, t, slot))
@@ -269,18 +291,29 @@
             def _():
                 start(down_copies(layer, 0, 1 - slot))
 
-            activate(lax.rem(t + n_gu - 1, n_gu), 1 - slot)
-            ga[slot] = dot(a[...], wa[slot])
-            ub[slot] = dot(a[...], wb[slot])
+            gate = dot(a[...], wa[slot])
+            up = dot(a[...], wb[slot])
+            for r in range(0, seq, ACT_ROWS):
+                act = jax.nn.gelu(gate[r:r + ACT_ROWS], approximate=True) * up[r:r + ACT_ROWS]
+                m[pl.ds(r, ACT_ROWS), block(t, TILE)] = act.astype(BF16)
 
         def gate_up_pair(i, _):
+            @pl.when(i == n_gu // 2 - 1)
+            def _():
+                finish_sum(1 - b, b)
+
             gate_up(2 * i, 0)
+
+            @pl.when((i == 0) & (b == 1))
+            def _():
+                chip_add(0, 1, n_down - 1)
+
             gate_up(2 * i + 1, 1)
             return 0
 
         lax.fori_loop(0, n_gu // 2, gate_up_pair, 0)
-        activate(n_gu - 1, 1)
-        finish_sum(1 - b, b)
+        finish_wait(1 - b, b)
+        next_norm = jnp.minimum(2 * layer + 1 + b, 2 * n_layers - 1)
 
         def down(t, slot):
             wait(down_copies(layer, t, slot))
@@ -301,6 +334,9 @@
             def _():
                 chip_add(b, 1, t - 2)
 
+            first = jnp.minimum(t * SPREAD_ROWS, seq - SPREAD_ROWS)
+            for r in range(0, SPREAD_ROWS, ACT_ROWS):
+                norm_rows(1 - b, next_norm, pl.ds(pl.multiple_of(first + r, ACT_ROWS), ACT_ROWS))
             part[b, :, block(t, TILE)] = (
                 dot(m[:, pl.ds(0, model)], wa[slot]) + dot(m[:, pl.ds(model, model)], wb[slot])
             ).astype(BF16)
@@ -311,18 +347,16 @@
             return 0
 
         lax.fori_loop(0, n_down // 2, down_pair, 0)
-        finish_wait(1 - b, b)
         send_part(b, n_down - 1).start()
         chip_add(b, 1, n_down - 2)
-        chip_add(b, 1, n_down - 1)
-
-    hidden_copies = [pltpu.make_async_copy(hidden.at[b], x.at[b], x_sem.at[b]) for b in range(prompts)]
-    start(hidden_copies)
+
+    hidden_copies[0].start()
     raw_start(w_query, 0)
+    hidden_copies[1].start()
     barrier = pltpu.get_barrier_semaphore()
     for device in (peer, far):
         pl.semaphore_signal(barrier, inc=1, device_id=device, device_id_type=pl.DeviceIdType.MESH)
-    wait(hidden_copies)
+    hidden_copies[0].wait()
     pl.semaphore_wait(barrier, 2)
 
     def layer_step(layer, _):
@@ -339,8 +373,9 @@
         return 0
 
     lax.fori_loop(0, n_layers, layer_step, 0)
-    out_copies = [pltpu.make_async_copy(x.at[b], h_out.at[b], x_sem.at[b]) for b in range(prompts)]
+    out_copies = [pltpu.make_async_copy(x.at[b], out, x_sem.at[b]) for b, out in enumerate((h_out0, h_out1))]
     out_copies[0].start()
+    chip_add(1, 1, n_down - 1)
     finish_sum(1, 1)
     finish_wait(1, 1)
     out_copies[1].start()
@@ -365,11 +400,13 @@
         vmem = pl.BlockSpec(memory_space=pltpu.VMEM)
         dma = pltpu.SemaphoreType.DMA
         cache = jax.ShapeDtypeStruct((n_layers, prompts, heads, seq, dim), BF16)
-        return pl.pallas_call(
+        gains = jnp.stack([norm_attn, norm_mlp], axis=1).reshape(2 * n_layers, model)
+        state = jax.ShapeDtypeStruct(hidden.shape[1:], BF16)
+        h0, h1, k_cache, v_cache = pl.pallas_call(
             kernel,
-            in_specs=[pl.BlockSpec(memory_space=pltpu.SMEM)] + [anywhere] * 8 + [vmem] * 4,
-            out_specs=[anywhere] * 3,
-            out_shape=[jax.ShapeDtypeStruct(hidden.shape, BF16), cache, cache],
+            in_specs=[pl.BlockSpec(memory_space=pltpu.SMEM)] + [anywhere] * 8 + [vmem] * 3,
+            out_specs=[anywhere] * 4,
+            out_shape=[state, state, cache, cache],
             scratch_shapes=[
                 pltpu.VMEM((prompts, seq, model), BF16),
                 pltpu.VMEM((seq, model), BF16),
@@ -391,8 +428,9 @@
             ),
         )(
             lengths, hidden, w_query, w_key, w_value, w_out.reshape(n_layers, inner, model), w_gate, w_up, w_down,
-            norm_attn, norm_mlp, cos_t, sin_t,
+            gains, cos_t, sin_t,
         )
+        return jnp.stack([h0, h1]), k_cache, v_cache
 
     return jax.shard_map(
         shard_body,

time: 468 us -> 424 us (0.906)
  Pallas kernels: 455 us -> 410 us
  other arithmetic: 1.75 us -> 7.04 us
    pallas_call x1, Pallas kernels: 455 us -> 410 us  [shard_body(): pl.pallas_call(kernel, in_specs=[pl.BlockSpec(memory_space=pltpu.SMEM)] +...]
    another operation x0 -> x2, other arithmetic: none -> 7.04 us  [the longest x1 6.26 us: shard_body(): return (jnp.stack([h0, h1]), k_cache, v_cache)]
    unnamed x7 -> x6, local copies, waits for them, and re-layouts: 10.5 us -> 5.72 us
where the time goes in v4:
time: 424 us
  Pallas kernels  410 us (97%)
  other arithmetic  7.04 us (2%)
  local copies, waits for them, and re-layouts  6.41 us (2%)
    pallas_call x1, Pallas kernels, shard_body(): pl.pallas_call(kernel, in_specs=[pl.BlockSpec(memory_space=pltpu.SMEM)] +...  410 us

profile of v4, /device:TPU:0, one launch (start us, length us, event | category | flops | bytes accessed | tf_op | source)
XLA Modules:
  0.0 424.2 jit_solution(8297113610122440983)
XLA Ops:
  0.6 0.8 pad_maximum_fusion.1
  1.4 0.7 reshape.13.gains
  2.1 410.0 %shard_map.148 = (bf16[512,3072]{1,0:T(8,128)(2,1)}, bf16[512,3072]{1,0:T(8,128)(2,1)}, bf16[2,2,4,512,256]{4,3,2,1,0:T(8,128)(2,1)}, bf16[2,2,4,512,256]{4,3,2,1,0:T(8,128)(2,1)}) custom-call(s32[2]{0:T(128)} %len_ref.1, bf16[2,512,3072]{2,1,0:T(8,128)(2,1)} %hidden.1, bf16[2,3072,4,256]{3,2,1,0:T(4,128)(2,1)} %w_query.1, bf16[2,3072,4,256]{3,2,1,0:T(4,128)(2,1)} %w_key.1, ...), custom_call_target="tpu_custom_call" | custom-call | tf_op jit(solution)/shard_map/pallas_call | solution.py:405
  412.2 0.0 copy-start.1
  412.2 6.3 %pad_maximum_fusion = bf16[2,512,3072]{2,1,0:T(8,128)(2,1)} fusion(bf16[1,512,3072]{2,1,0:T(8,128)(2,1)} %bitcast.7, bf16[1,512,3072]{2,1,0:T(8,128)(2,1)} %bitcast.6), kind=kLoop, calls=%fused_computation | loop fusion | flops 3145728 | bytes 12582912 | tf_op jit(solution)/shard_map/stack | solution.py:433
  418.4 0.0 copy-done.1
  418.4 0.0 copy-start
  418.4 2.1 copy.19
  420.6 1.6 copy-done
  422.1 2.0 copy.20
  (1 shorter events, 0.0 us)
Async XLA Ops:
  412.2 6.3 %copy-start.1 = (bf16[2,2,4,512,256]{4,3,2,1,0:T(8,128)(2,1)S(1)}, bf16[2,2,4,512,256]{4,3,2,1,0:T(8,128)(2,1)}, u32[]{:S(2)}) copy-start(bf16[2,2,4,512,256]{4,3,2,1,0:T(8,128)(2,1)} %get-tuple-element.15) | copy-start | bytes 12582916
  418.4 3.7 copy-start

commit v5 on v4

--- a/solution.py
+++ b/solution.py
@@ -11,7 +11,7 @@
 TILE = 512
 NORM_ROWS = 64
 ACT_ROWS = 16
-SPREAD_ROWS = 96
+SPREAD_ROWS = 176
 F32, BF16 = jnp.float32, jnp.bfloat16
 
 
@@ -46,49 +46,73 @@
     core = lax.rem(me, 2)
     peer = {"tp": me + 1 - 2 * core}
     far = {"tp": lax.rem(me + 2, 4)}
-    own = block(core, half)
-    other = block(1 - core, half)
+    own_row = core * half
+    other_row = (1 - core) * half
+
+    def rows_from(start, size):
+        return pl.ds(pl.multiple_of(start, 128), size)
+
+    def piece(stage, t):
+        if stage == 0:
+            j = lax.div(jnp.int32(t), 3)
+            return j * (half // 2), half // 2, block(t - 3 * j, 2 * TILE)
+        return 0, half, block(t, TILE)
 
     def remote(src, dst, send_sem, recv_sem, device):
         return pltpu.make_async_remote_copy(src, dst, send_sem, recv_sem, device_id=device, device_id_type=pl.DeviceIdType.MESH)
 
-    def send_part(b, t):
-        c = block(t, TILE)
-        return remote(part.at[b, other, c], recv1.at[b, :, c], s1.at[b, t], r1.at[b, t], peer)
+    def send_part(b, stage, t):
+        row, n, c = piece(stage, t)
+        return remote(
+            part.at[b, rows_from(other_row + row, n), c], recv1.at[b, rows_from(row, n), c], s1.at[b, t], r1.at[b, t], peer
+        )
 
     def send_far(b, stage, t):
-        c = block(t, TILE)
-        return remote(part.at[b, own, c], recv2.at[stage, b, :, c], s2.at[b, t], r2.at[stage, b, t], far)
-
-    def send_x(b, t):
-        c = block(t, TILE)
-        return remote(x.at[b, own, c], x.at[b, own, c], s3.at[b, t], r3.at[b, t], peer)
+        row, n, c = piece(stage, t)
+        return remote(
+            part.at[b, rows_from(own_row + row, n), c], recv2.at[stage, b, rows_from(row, n), c],
+            s2.at[b, t], r2.at[stage, b, t], far,
+        )
+
+    def send_x(b, stage, t):
+        row, n, c = piece(stage, t)
+        rows = rows_from(own_row + row, n)
+        return remote(x.at[b, rows, c], x.at[b, rows, c], s3.at[b, t], r3.at[b, t], peer)
 
     def chip_add(b, stage, t):
-        c = block(t, TILE)
-        send_part(b, t).wait_recv()
-        part[b, own, c] = (part[b, own, c].astype(F32) + recv1[b, :, c].astype(F32)).astype(BF16)
+        row, n, c = piece(stage, t)
+        rows = rows_from(own_row + row, n)
+        send_part(b, stage, t).wait_recv()
+        part[b, rows, c] = (part[b, rows, c].astype(F32) + recv1[b, rows_from(row, n), c].astype(F32)).astype(BF16)
         send_far(b, stage, t).start()
 
-    def finish_sum(b, stage):
+    def chip_adds(b, stage, first, last):
         def body(t, _):
-            c = block(t, TILE)
+            chip_add(b, stage, t)
+            return 0
+
+        lax.fori_loop(first, last, body, 0)
+
+    def finish_sum(b, stage, first, last):
+        def body(t, _):
+            row, n, c = piece(stage, t)
+            rows = rows_from(own_row + row, n)
             send_far(b, stage, t).wait_recv()
-            total = part[b, own, c].astype(F32) + recv2[stage, b, :, c].astype(F32)
-            x[b, own, c] = (x[b, own, c].astype(F32) + total).astype(BF16)
-            send_x(b, t).start()
-            return 0
-
-        lax.fori_loop(0, n_down, body, 0)
-
-    def finish_wait(b, stage):
+            total = part[b, rows, c].astype(F32) + recv2[stage, b, rows_from(row, n), c].astype(F32)
+            x[b, rows, c] = (x[b, rows, c].astype(F32) + total).astype(BF16)
+            send_x(b, stage, t).start()
+            return 0
+
+        lax.fori_loop(first, last, body, 0)
+
+    def finish_wait(b, stage, first, last):
         def body(t, _):
-            send_part(b, t).wait_send()
+            send_part(b, stage, t).wait_send()
             send_far(b, stage, t).wait_send()
-            send_x(b, t).wait()
-            return 0
-
-        lax.fori_loop(0, n_down, body, 0)
+            send_x(b, stage, t).wait()
+            return 0
+
+        lax.fori_loop(first, last, body, 0)
 
     def norm_rows(b, which, rows):
         v = x[b, rows, :].astype(F32)
@@ -110,19 +134,19 @@
         for c in range(n_raw):
             raw_copy(w, layer, c).start()
 
-    def raw_wait(w, layer):
+    def relayout(slot, w, layer, then=None):
         for c in range(n_raw):
             raw_copy(w, layer, c).wait()
-
-    def relayout(slot):
         for c in range(n_raw):
             rows = pl.ds(c * raw_rows, raw_rows)
             v = raw[rows].reshape(raw_rows, inner)
             wa[slot, rows, :] = v[:, :TILE]
             wb[slot, rows, :] = v[:, TILE:]
+            if then is not None:
+                raw_copy(then, layer, c).start()
 
     def out_copy(layer, t):
-        dst = (wa if t < 3 else wb).at[1, pl.ds((t % 3) * inner, inner), :]
+        dst = (wb if t % 2 else wa).at[1, pl.ds((t // 2) * inner, inner), :]
         return pltpu.make_async_copy(w_out.at[layer, :, pl.ds(t * TILE, TILE)], dst, wo_sem.at[t])
 
     def gu_copies(layer, t, slot):
@@ -190,30 +214,24 @@
         def _():
             norm(b, 2 * layer)
 
-        raw_wait(w_query, layer)
-        relayout(0)
-        raw_start(w_key, layer)
+        @pl.when(b == 1)
+        def _():
+            chip_adds(0, 0, 2, n_down)
+
+        relayout(0, w_query, layer, w_key)
         ga[0] = dot(a[...], wa[0])
         ga[1] = dot(a[...], wb[0])
 
-        @pl.when(b == 1)
-        def _():
-            chip_add(0, 0, 2)
-            chip_add(0, 0, 5)
-
         @pl.when((b == 0) & (layer > 0))
         def _():
             chip_add(1, 1, n_down - 1)
 
-        raw_wait(w_key, layer)
-        relayout(1)
-        raw_start(w_value, layer)
+        relayout(1, w_key, layer, w_value)
         ub[0] = dot(a[...], wa[1])
         ub[1] = dot(a[...], wb[1])
         for t in range(n_down):
             out_copy(layer, t).start()
-        raw_wait(w_value, layer)
-        relayout(0)
+        relayout(0, w_value, layer)
         m[:, pl.ds(0, TILE)] = dot(a[...], wa[0]).astype(BF16)
         m[:, pl.ds(TILE, TILE)] = dot(a[...], wb[0]).astype(BF16)
 
@@ -236,86 +254,117 @@
 
         @pl.when((b == 0) & (layer > 0))
         def _():
-            finish_sum(1, 1)
+            finish_sum(1, 1, 0, n_down)
 
         for t in range(n_down):
             out_copy(layer, t).wait()
         o_cols = pl.ds(2 * inner, inner)
 
+        def send_both(i):
+            send_part(b, 0, i).start()
+            send_part(b, 0, i + 3).start()
+
         def project(i, _):
             @pl.when(i > 0)
             def _():
-                send_part(b, i - 1).start()
-                send_part(b, i + 2).start()
-
-            part[b, :, block(i, TILE)] = dot(m[:, o_cols], wa[1, block(i, inner), :]).astype(BF16)
-            part[b, :, block(i + 3, TILE)] = dot(m[:, o_cols], wb[1, block(i, inner), :]).astype(BF16)
+                send_both(i - 1)
+
+            part[b, :, block(2 * i, TILE)] = dot(m[:, o_cols], wa[1, block(i, inner), :]).astype(BF16)
+            part[b, :, block(2 * i + 1, TILE)] = dot(m[:, o_cols], wb[1, block(i, inner), :]).astype(BF16)
             return 0
 
         lax.fori_loop(0, 3, project, 0)
         for h in range(heads):
             wait(cache_copies(layer, b, h))
-        send_part(b, 2).start()
-        send_part(b, 5).start()
-        for t in (0, 3, 1, 4):
-            chip_add(b, 0, t)
+        send_both(2)
+        chip_adds(b, 0, 0, 2)
 
         @pl.when((b == 0) & (layer > 0))
         def _():
-            finish_wait(1, 1)
-
-        @pl.when(b == 1)
-        def _():
-            chip_add(1, 0, 2)
-            chip_add(1, 0, 5)
-            finish_sum(0, 0)
-            finish_wait(0, 0)
+            finish_wait(1, 1, 0, n_down)
 
     def mlp_phase(layer, b):
         @pl.when((b == 1) & (layer + 1 < n_layers))
         def _():
             raw_start(w_query, layer + 1)
 
+        def gate_up(t, after, slot, h):
+            wait(gu_copies(layer, t, slot))
+
+            @pl.when(after < n_gu)
+            def _():
+                start(gu_copies(layer, after, 1 - slot))
+
+            @pl.when(after == n_gu)
+            def _():
+                start(down_copies(layer, 0, 1 - slot))
+
+            if h is None:
+                lhs = a[...]
+                starts = range(0, seq, ACT_ROWS)
+            else:
+                quarter = half // 2
+                lows = [rows_from(i * half + h * quarter, quarter) for i in range(2)]
+                lhs = jnp.concatenate([a[r, :] for r in lows], axis=0)
+                starts = [i * half + h * quarter + r for i in range(2) for r in range(0, quarter, ACT_ROWS)]
+            gate = dot(lhs, wa[slot])
+            up = dot(lhs, wb[slot])
+            for i, row in enumerate(starts):
+                r = i * ACT_ROWS
+                act = jax.nn.gelu(gate[r:r + ACT_ROWS], approximate=True) * up[r:r + ACT_ROWS]
+                m[pl.ds(row if h is None else pl.multiple_of(row, ACT_ROWS), ACT_ROWS), block(t, TILE)] = act.astype(BF16)
+
+        def norm_half(h):
+            def body(i, _):
+                j = lax.div(i, 2)
+                norm_rows(0, 2 * layer + 1, pl.ds(pl.multiple_of(j * half + h * (half // 2) + (i - 2 * j) * NORM_ROWS, NORM_ROWS), NORM_ROWS))
+                return 0
+
+            lax.fori_loop(0, 4, body, 0)
+
         @pl.when(b == 0)
         def _():
-            norm(b, 2 * layer + 1)
-
-        def gate_up(t, slot):
-            wait(gu_copies(layer, t, slot))
-
-            @pl.when(t + 1 < n_gu)
-            def _():
-                start(gu_copies(layer, t + 1, 1 - slot))
-
-            @pl.when(t + 1 == n_gu)
-            def _():
-                start(down_copies(layer, 0, 1 - slot))
-
-            gate = dot(a[...], wa[slot])
-            up = dot(a[...], wb[slot])
-            for r in range(0, seq, ACT_ROWS):
-                act = jax.nn.gelu(gate[r:r + ACT_ROWS], approximate=True) * up[r:r + ACT_ROWS]
-                m[pl.ds(r, ACT_ROWS), block(t, TILE)] = act.astype(BF16)
-
-        def gate_up_pair(i, _):
-            @pl.when(i == n_gu // 2 - 1)
-            def _():
-                finish_sum(1 - b, b)
-
-            gate_up(2 * i, 0)
-
-            @pl.when((i == 0) & (b == 1))
-            def _():
-                chip_add(0, 1, n_down - 1)
-
-            gate_up(2 * i + 1, 1)
-            return 0
-
-        lax.fori_loop(0, n_gu // 2, gate_up_pair, 0)
-        finish_wait(1 - b, b)
+            finish_sum(0, 0, 0, 3)
+            chip_adds(1, 0, 2, n_down)
+            finish_wait(0, 0, 0, 3)
+            norm_half(0)
+
+            def step(u, _):
+                h = lax.div(u, n_gu)
+
+                @pl.when(u == n_gu - 1)
+                def _():
+                    finish_sum(0, 0, 3, n_down)
+
+                @pl.when(u == n_gu)
+                def _():
+                    finish_wait(0, 0, 3, n_down)
+                    norm_half(1)
+
+                t = u - h * n_gu
+                last = u == 2 * n_gu - 1
+                after = jnp.where(last, n_gu, lax.rem(u + 1, n_gu))
+                gate_up(t, after, lax.rem(u, 2), h)
+                return 0
+
+            lax.fori_loop(0, 2 * n_gu, step, 0)
+
+        @pl.when(b == 1)
+        def _():
+            def step(t, _):
+                @pl.when(t == 1)
+                def _():
+                    chip_add(0, 1, n_down - 1)
+
+                gate_up(t, t + 1, lax.rem(t, 2), None)
+                return 0
+
+            lax.fori_loop(0, n_gu, step, 0)
+
         next_norm = jnp.minimum(2 * layer + 1 + b, 2 * n_layers - 1)
 
-        def down(t, slot):
+        def down(t, with_norm):
+            slot = lax.rem(t, 2)
             wait(down_copies(layer, t, slot))
 
             @pl.when(t + 1 < n_down)
@@ -328,26 +377,48 @@
 
             @pl.when(t > 0)
             def _():
-                send_part(b, t - 1).start()
+                send_part(b, 1, t - 1).start()
 
             @pl.when(t > 1)
             def _():
                 chip_add(b, 1, t - 2)
 
-            first = jnp.minimum(t * SPREAD_ROWS, seq - SPREAD_ROWS)
-            for r in range(0, SPREAD_ROWS, ACT_ROWS):
-                norm_rows(1 - b, next_norm, pl.ds(pl.multiple_of(first + r, ACT_ROWS), ACT_ROWS))
+            if with_norm:
+                first = jnp.minimum((t - 3) * SPREAD_ROWS, seq - SPREAD_ROWS)
+                for r in range(0, SPREAD_ROWS, ACT_ROWS):
+                    norm_rows(1 - b, next_norm, pl.ds(pl.multiple_of(first + r, ACT_ROWS), ACT_ROWS))
             part[b, :, block(t, TILE)] = (
                 dot(m[:, pl.ds(0, model)], wa[slot]) + dot(m[:, pl.ds(model, model)], wb[slot])
             ).astype(BF16)
 
-        def down_pair(i, _):
-            down(2 * i, 0)
-            down(2 * i + 1, 1)
-            return 0
-
-        lax.fori_loop(0, n_down // 2, down_pair, 0)
-        send_part(b, n_down - 1).start()
+        def down_plain(t, _):
+            @pl.when((t == 2) & (b == 0))
+            def _():
+                finish_sum(1, 0, 0, n_down)
+
+            @pl.when((t == 2) & (b == 1))
+            def _():
+                finish_sum(0, 1, 0, n_down)
+
+            down(t, False)
+            return 0
+
+        def down_norm(t, _):
+            down(t, True)
+            return 0
+
+        lax.fori_loop(0, 3, down_plain, 0)
+
+        @pl.when(b == 0)
+        def _():
+            finish_wait(1, 0, 0, n_down)
+
+        @pl.when(b == 1)
+        def _():
+            finish_wait(0, 1, 0, n_down)
+
+        lax.fori_loop(3, n_down, down_norm, 0)
+        send_part(b, 1, n_down - 1).start()
         chip_add(b, 1, n_down - 2)
 
     hidden_copies[0].start()
@@ -376,8 +447,8 @@
     out_copies = [pltpu.make_async_copy(x.at[b], out, x_sem.at[b]) for b, out in enumerate((h_out0, h_out1))]
     out_copies[0].start()
     chip_add(1, 1, n_down - 1)
-    finish_sum(1, 1)
-    finish_wait(1, 1)
+    finish_sum(1, 1, 0, n_down)
+    finish_wait(1, 1, 0, n_down)
     out_copies[1].start()
     wait(out_copies)
 

time: 424 us -> 450 us (1.061)
  Pallas kernels: 410 us -> 435 us
    pallas_call x1, Pallas kernels: 410 us -> 435 us  [shard_body(): pl.pallas_call(kernel, in_specs=[pl.BlockSpec(memory_space=pltpu.SMEM)] +...]
where the time goes in v5:
time: 450 us; the launch traced here: 449 us
  Pallas kernels  435 us (97%)
  other arithmetic  7.04 us (2%)
  local copies, waits for them, and re-layouts  6.41 us (1%)
    pallas_call x1, Pallas kernels, shard_body(): pl.pallas_call(kernel, in_specs=[pl.BlockSpec(memory_space=pltpu.SMEM)] +...  435 us

profile of v5, /device:TPU:0, one launch (start us, length us, event | category | flops | bytes accessed | tf_op | source)
XLA Modules:
  0.0 449.5 jit_solution(9622104551026666449)
XLA Ops:
  0.6 0.8 pad_maximum_fusion.1
  1.4 0.7 reshape.13.gains
  2.1 435.3 %shard_map.148 = (bf16[512,3072]{1,0:T(8,128)(2,1)}, bf16[512,3072]{1,0:T(8,128)(2,1)}, bf16[2,2,4,512,256]{4,3,2,1,0:T(8,128)(2,1)}, bf16[2,2,4,512,256]{4,3,2,1,0:T(8,128)(2,1)}) custom-call(s32[2]{0:T(128)} %len_ref.1, bf16[2,512,3072]{2,1,0:T(8,128)(2,1)} %hidden.1, bf16[2,3072,4,256]{3,2,1,0:T(4,128)(2,1)} %w_query.1, bf16[2,3072,4,256]{3,2,1,0:T(4,128)(2,1)} %w_key.1, ...), custom_call_target="tpu_custom_call" | custom-call | tf_op jit(solution)/shard_map/pallas_call | solution.py:476
  437.5 0.0 copy-start.1
  437.5 6.3 %pad_maximum_fusion = bf16[2,512,3072]{2,1,0:T(8,128)(2,1)} fusion(bf16[1,512,3072]{2,1,0:T(8,128)(2,1)} %bitcast.7, bf16[1,512,3072]{2,1,0:T(8,128)(2,1)} %bitcast.6), kind=kLoop, calls=%fused_computation | loop fusion | flops 3145728 | bytes 12582912 | tf_op jit(solution)/shard_map/stack | solution.py:504
  443.7 0.0 copy-done.1
  443.7 0.0 copy-start
  443.7 2.1 copy.19
  445.9 1.6 copy-done
  447.4 2.0 copy.20
  (1 shorter events, 0.0 us)
Async XLA Ops:
  437.5 6.3 %copy-start.1 = (bf16[2,2,4,512,256]{4,3,2,1,0:T(8,128)(2,1)S(1)}, bf16[2,2,4,512,256]{4,3,2,1,0:T(8,128)(2,1)}, u32[]{:S(2)}) copy-start(bf16[2,2,4,512,256]{4,3,2,1,0:T(8,128)(2,1)} %get-tuple-element.15) | copy-start | bytes 12582916
  443.7 3.7 copy-start

commit v6 on v5

--- a/solution.py
+++ b/solution.py
@@ -9,6 +9,7 @@
 RMS_EPS = 1e-6
 ROPE_BASE = 10000.0
 TILE = 512
+SLOTS = 3
 NORM_ROWS = 64
 ACT_ROWS = 16
 SPREAD_ROWS = 176
@@ -27,10 +28,10 @@
 
 
 def kernel(
-    len_ref, hidden, w_query, w_key, w_value, w_out, w_gate, w_up, w_down, gains, cos_ref, sin_ref,
+    len_ref, hidden, w_query, w_key, w_value, w_out, w_gate, w_up, w_down, gain_attn, gain_mlp, cos_ref, sin_ref,
     h_out0, h_out1, k_cache, v_cache,
-    x, a, m, wa, wb, raw, ga, ub, part, recv1, recv2,
-    x_sem, wa_sem, wb_sem, raw_sem, wo_sem, kc_sem, vc_sem, s1, r1, s2, r2, s3, r3,
+    x, a, m, wa, wb, raw, part, recv1, recv2, gains,
+    x_sem, wa_sem, wb_sem, raw_sem, wo_sem, kc_sem, vc_sem, s1, r1, s2, r2, s3, r3, credit,
 ):
     n_layers, model, heads, dim = w_query.shape
     prompts, seq, _ = hidden.shape
@@ -70,8 +71,8 @@
     def send_far(b, stage, t):
         row, n, c = piece(stage, t)
         return remote(
-            part.at[b, rows_from(own_row + row, n), c], recv2.at[stage, b, rows_from(row, n), c],
-            s2.at[b, t], r2.at[stage, b, t], far,
+            part.at[b, rows_from(own_row + row, n), c], recv2.at[b, rows_from(row, n), c],
+            s2.at[b, t], r2.at[b, t], far,
         )
 
     def send_x(b, stage, t):
@@ -98,12 +99,14 @@
             row, n, c = piece(stage, t)
             rows = rows_from(own_row + row, n)
             send_far(b, stage, t).wait_recv()
-            total = part[b, rows, c].astype(F32) + recv2[stage, b, rows_from(row, n), c].astype(F32)
+            total = part[b, rows, c].astype(F32) + recv2[b, rows_from(row, n), c].astype(F32)
             x[b, rows, c] = (x[b, rows, c].astype(F32) + total).astype(BF16)
             send_x(b, stage, t).start()
             return 0
 
         lax.fori_loop(first, last, body, 0)
+        if last == n_down:
+            pl.semaphore_signal(credit.at[b], inc=1, device_id=far, device_id_type=pl.DeviceIdType.MESH)
 
     def finish_wait(b, stage, first, last):
         def body(t, _):
@@ -146,7 +149,7 @@
                 raw_copy(then, layer, c).start()
 
     def out_copy(layer, t):
-        dst = (wb if t % 2 else wa).at[1, pl.ds((t // 2) * inner, inner), :]
+        dst = (wb if t % 2 else wa).at[2, pl.ds((t // 2) * inner, inner), :]
         return pltpu.make_async_copy(w_out.at[layer, :, pl.ds(t * TILE, TILE)], dst, wo_sem.at[t])
 
     def gu_copies(layer, t, slot):
@@ -180,18 +183,20 @@
             pltpu.make_async_copy(m.at[:, block(h, dim)], v_cache.at[layer, b, h], vc_sem.at[h]),
         )
 
+    def rotate(v, first, scale):
+        for r in range(0, seq, ACT_ROWS):
+            rows = pl.ds(r, ACT_ROWS)
+            cos_t, sin_t = cos_ref[rows, :], sin_ref[rows, :]
+            for c in range(0, TILE, dim):
+                lo, hi = v[r:r + ACT_ROWS, c:c + half_dim], v[r:r + ACT_ROWS, c + half_dim:c + dim]
+                for d, w in ((0, lo * cos_t - hi * sin_t), (half_dim, hi * cos_t + lo * sin_t)):
+                    w = w if scale is None else w * scale
+                    m[rows, pl.ds(first + c + d, half_dim)] = w.astype(BF16)
+
     def head(b, i, j):
         h = 2 * i + j
-        lanes = slice(j * dim, (j + 1) * dim)
-        cos_t, sin_t = cos_ref[...], sin_ref[...]
-
-        def rope(v):
-            lo, hi = v[:, :half_dim], v[:, half_dim:]
-            return jnp.concatenate([lo * cos_t - hi * sin_t, hi * cos_t + lo * sin_t], axis=-1)
-
-        q = (rope(ga[i, :, lanes]) * (dim ** -0.5)).astype(BF16)
-        k = rope(ub[i, :, lanes]).astype(BF16)
-        m[:, block(heads + h, dim)] = k
+        q = m[:, block(3 * heads + h, dim)]
+        k = m[:, block(heads + h, dim)]
         for r in range(2):
             keys = (r + 1) * half
             v = m[pl.ds(0, keys), block(h, dim)]
@@ -219,16 +224,16 @@
             chip_adds(0, 0, 2, n_down)
 
         relayout(0, w_query, layer, w_key)
-        ga[0] = dot(a[...], wa[0])
-        ga[1] = dot(a[...], wb[0])
+        rotate(dot(a[...], wa[0]), 3 * inner, dim ** -0.5)
+        rotate(dot(a[...], wb[0]), 3 * inner + TILE, dim ** -0.5)
 
         @pl.when((b == 0) & (layer > 0))
         def _():
             chip_add(1, 1, n_down - 1)
 
         relayout(1, w_key, layer, w_value)
-        ub[0] = dot(a[...], wa[1])
-        ub[1] = dot(a[...], wb[1])
+        rotate(dot(a[...], wa[1]), inner, None)
+        rotate(dot(a[...], wb[1]), inner + TILE, None)
         for t in range(n_down):
             out_copy(layer, t).start()
         relayout(0, w_value, layer)
@@ -242,6 +247,7 @@
         @pl.when(b == 1)
         def _():
             start(gu_copies(layer, 0, 0))
+            start(gu_copies(layer, 1, 1))
 
         def two_heads(i, _):
             head(b, i, 0)
@@ -269,14 +275,19 @@
             def _():
                 send_both(i - 1)
 
-            part[b, :, block(2 * i, TILE)] = dot(m[:, o_cols], wa[1, block(i, inner), :]).astype(BF16)
-            part[b, :, block(2 * i + 1, TILE)] = dot(m[:, o_cols], wb[1, block(i, inner), :]).astype(BF16)
+            part[b, :, block(2 * i, TILE)] = dot(m[:, o_cols], wa[2, block(i, inner), :]).astype(BF16)
+            part[b, :, block(2 * i + 1, TILE)] = dot(m[:, o_cols], wb[2, block(i, inner), :]).astype(BF16)
             return 0
 
         lax.fori_loop(0, 3, project, 0)
         for h in range(heads):
             wait(cache_copies(layer, b, h))
         send_both(2)
+
+        @pl.when(layer > 0)
+        def _():
+            pl.semaphore_wait(credit.at[b], 1)
+
         chip_adds(b, 0, 0, 2)
 
         @pl.when((b == 0) & (layer > 0))
@@ -288,16 +299,19 @@
         def _():
             raw_start(w_query, layer + 1)
 
-        def gate_up(t, after, slot, h):
+        def gate_up(u, steps, h):
+            slot, ahead = lax.rem(u, SLOTS), u + 2
+            slot_ahead = lax.rem(ahead, SLOTS)
+            t = lax.rem(u, n_gu)
             wait(gu_copies(layer, t, slot))
 
-            @pl.when(after < n_gu)
-            def _():
-                start(gu_copies(layer, after, 1 - slot))
-
-            @pl.when(after == n_gu)
-            def _():
-                start(down_copies(layer, 0, 1 - slot))
+            @pl.when(ahead < steps)
+            def _():
+                start(gu_copies(layer, lax.rem(ahead, n_gu), slot_ahead))
+
+            @pl.when(ahead >= steps)
+            def _():
+                start(down_copies(layer, ahead - steps, slot_ahead))
 
             if h is None:
                 lhs = a[...]
@@ -341,10 +355,7 @@
                     finish_wait(0, 0, 3, n_down)
                     norm_half(1)
 
-                t = u - h * n_gu
-                last = u == 2 * n_gu - 1
-                after = jnp.where(last, n_gu, lax.rem(u + 1, n_gu))
-                gate_up(t, after, lax.rem(u, 2), h)
+                gate_up(u, 2 * n_gu, h)
                 return 0
 
             lax.fori_loop(0, 2 * n_gu, step, 0)
@@ -356,7 +367,7 @@
                 def _():
                     chip_add(0, 1, n_down - 1)
 
-                gate_up(t, t + 1, lax.rem(t, 2), None)
+                gate_up(t, n_gu, None)
                 return 0
 
             lax.fori_loop(0, n_gu, step, 0)
@@ -364,20 +375,25 @@
         next_norm = jnp.minimum(2 * layer + 1 + b, 2 * n_layers - 1)
 
         def down(t, with_norm):
-            slot = lax.rem(t, 2)
+            slot, ahead = lax.rem(t, SLOTS), t + 2
+            slot_ahead = lax.rem(ahead, SLOTS)
             wait(down_copies(layer, t, slot))
 
-            @pl.when(t + 1 < n_down)
-            def _():
-                start(down_copies(layer, t + 1, 1 - slot))
-
-            @pl.when((t + 1 == n_down) & (b == 0))
-            def _():
-                start(gu_copies(layer, 0, 1 - slot))
+            @pl.when(ahead < n_down)
+            def _():
+                start(down_copies(layer, ahead, slot_ahead))
+
+            @pl.when((ahead >= n_down) & (b == 0))
+            def _():
+                start(gu_copies(layer, ahead - n_down, slot_ahead))
 
             @pl.when(t > 0)
             def _():
                 send_part(b, 1, t - 1).start()
+
+            @pl.when(t == 2)
+            def _():
+                pl.semaphore_wait(credit.at[b], 1)
 
             @pl.when(t > 1)
             def _():
@@ -427,6 +443,9 @@
     barrier = pltpu.get_barrier_semaphore()
     for device in (peer, far):
         pl.semaphore_signal(barrier, inc=1, device_id=device, device_id_type=pl.DeviceIdType.MESH)
+    for i in range(n_layers):
+        gains[pl.ds(2 * i, 1), :] = gain_attn[pl.ds(i, 1), :]
+        gains[pl.ds(2 * i + 1, 1), :] = gain_mlp[pl.ds(i, 1), :]
     hidden_copies[0].wait()
     pl.semaphore_wait(barrier, 2)
 
@@ -450,6 +469,8 @@
     finish_sum(1, 1, 0, n_down)
     finish_wait(1, 1, 0, n_down)
     out_copies[1].start()
+    for b in range(prompts):
+        pl.semaphore_wait(credit.at[b], 1)
     wait(out_copies)
 
 
@@ -471,35 +492,33 @@
         vmem = pl.BlockSpec(memory_space=pltpu.VMEM)
         dma = pltpu.SemaphoreType.DMA
         cache = jax.ShapeDtypeStruct((n_layers, prompts, heads, seq, dim), BF16)
-        gains = jnp.stack([norm_attn, norm_mlp], axis=1).reshape(2 * n_layers, model)
         state = jax.ShapeDtypeStruct(hidden.shape[1:], BF16)
         h0, h1, k_cache, v_cache = pl.pallas_call(
             kernel,
-            in_specs=[pl.BlockSpec(memory_space=pltpu.SMEM)] + [anywhere] * 8 + [vmem] * 3,
+            in_specs=[pl.BlockSpec(memory_space=pltpu.SMEM)] + [anywhere] * 8 + [vmem] * 4,
             out_specs=[anywhere] * 4,
             out_shape=[state, state, cache, cache],
             scratch_shapes=[
                 pltpu.VMEM((prompts, seq, model), BF16),
                 pltpu.VMEM((seq, model), BF16),
                 pltpu.VMEM((seq, width), BF16),
-                pltpu.VMEM((2, model, TILE), BF16),
-                pltpu.VMEM((2, model, TILE), BF16),
+                pltpu.VMEM((SLOTS, model, TILE), BF16),
+                pltpu.VMEM((SLOTS, model, TILE), BF16),
                 pltpu.VMEM((model, heads, dim), BF16),
-                pltpu.VMEM((2, seq, TILE), F32),
-                pltpu.VMEM((2, seq, TILE), F32),
                 pltpu.VMEM((prompts, seq, model), BF16),
                 pltpu.VMEM((prompts, half, model), BF16),
-                pltpu.VMEM((2, prompts, half, model), BF16),
-                dma((prompts,)), dma((2,)), dma((2,)), dma((4,)), dma((n_down,)), dma((heads,)), dma((heads,)),
-                dma((prompts, n_down)), dma((prompts, n_down)), dma((prompts, n_down)), dma((2, prompts, n_down)),
-                dma((prompts, n_down)), dma((prompts, n_down)),
+                pltpu.VMEM((prompts, half, model), BF16),
+                pltpu.VMEM((2 * n_layers, model), F32),
+                dma((prompts,)), dma((SLOTS,)), dma((SLOTS,)), dma((4,)), dma((n_down,)), dma((heads,)), dma((heads,)),
+                dma((prompts, n_down)), dma((prompts, n_down)), dma((prompts, n_down)), dma((prompts, n_down)),
+                dma((prompts, n_down)), dma((prompts, n_down)), pltpu.SemaphoreType.REGULAR((prompts,)),
             ],
             compiler_params=pltpu.CompilerParams(
                 collective_id=0, has_side_effects=True, vmem_limit_bytes=63 * 1024 * 1024
             ),
         )(
             lengths, hidden, w_query, w_key, w_value, w_out.reshape(n_layers, inner, model), w_gate, w_up, w_down,
-            gains, cos_t, sin_t,
+            norm_attn, norm_mlp, cos_t, sin_t,
         )
         return jnp.stack([h0, h1]), k_cache, v_cache
 

time: 450 us -> 401 us (0.89)
  Pallas kernels: 435 us -> 388 us
    pallas_call x1, Pallas kernels: 435 us -> 388 us  [shard_body(): pl.pallas_call(kernel, in_specs=[pl.BlockSpec(memory_space=pltpu.SMEM)] +...]
where the time goes in v6:
time: 401 us
  Pallas kernels  388 us (97%)
  other arithmetic  6.26 us (2%)
  local copies, waits for them, and re-layouts  5.72 us (1%)
    pallas_call x1, Pallas kernels, shard_body(): pl.pallas_call(kernel, in_specs=[pl.BlockSpec(memory_space=pltpu.SMEM)] +...  388 us

profile of v6, /device:TPU:0, one launch (start us, length us, event | category | flops | bytes accessed | tf_op | source)
XLA Modules:
  0.0 401.0 jit_solution(15287517088844308532)
XLA Ops:
  0.6 388.4 %shard_map.148 = (bf16[512,3072]{1,0:T(8,128)(2,1)}, bf16[512,3072]{1,0:T(8,128)(2,1)}, bf16[2,2,4,512,256]{4,3,2,1,0:T(8,128)(2,1)}, bf16[2,2,4,512,256]{4,3,2,1,0:T(8,128)(2,1)}) custom-call(s32[2]{0:T(128)} %len_ref.1, bf16[2,512,3072]{2,1,0:T(8,128)(2,1)} %hidden.1, bf16[2,3072,4,256]{3,2,1,0:T(4,128)(2,1)} %w_query.1, bf16[2,3072,4,256]{3,2,1,0:T(4,128)(2,1)} %w_key.1, ...), custom_call_target="tpu_custom_call" | custom-call | tf_op jit(solution)/shard_map/pallas_call | solution.py:496
  389.0 0.0 copy-start.1
  389.0 6.3 %pad_maximum_fusion = bf16[2,512,3072]{2,1,0:T(8,128)(2,1)} fusion(bf16[1,512,3072]{2,1,0:T(8,128)(2,1)} %bitcast.5, bf16[1,512,3072]{2,1,0:T(8,128)(2,1)} %bitcast.4), kind=kLoop, calls=%fused_computation | loop fusion | flops 3145728 | bytes 12582912 | tf_op jit(solution)/shard_map/stack | solution.py:523
  395.3 0.0 copy-done.1
  395.3 0.0 copy-start
  395.3 2.1 copy.18
  397.4 1.6 copy-done
  399.0 2.0 copy.19
Async XLA Ops:
  389.0 6.3 %copy-start.1 = (bf16[2,2,4,512,256]{4,3,2,1,0:T(8,128)(2,1)S(1)}, bf16[2,2,4,512,256]{4,3,2,1,0:T(8,128)(2,1)}, u32[]{:S(2)}) copy-start(bf16[2,2,4,512,256]{4,3,2,1,0:T(8,128)(2,1)} %get-tuple-element.15) | copy-start | bytes 12582916
  395.3 3.7 copy-start

commit v7 on v6

--- a/solution.py
+++ b/solution.py
@@ -299,15 +299,15 @@
         def _():
             raw_start(w_query, layer + 1)
 
-        def gate_up(u, steps, h):
+        def gate_up(u, steps, tile, h):
             slot, ahead = lax.rem(u, SLOTS), u + 2
             slot_ahead = lax.rem(ahead, SLOTS)
-            t = lax.rem(u, n_gu)
+            t = tile(u)
             wait(gu_copies(layer, t, slot))
 
             @pl.when(ahead < steps)
             def _():
-                start(gu_copies(layer, lax.rem(ahead, n_gu), slot_ahead))
+                start(gu_copies(layer, tile(ahead), slot_ahead))
 
             @pl.when(ahead >= steps)
             def _():
@@ -343,22 +343,37 @@
             finish_wait(0, 0, 0, 3)
             norm_half(0)
 
+            split = 3 * n_gu // 4
+            steps = n_gu + split
+
+            def tile(u):
+                group = lax.div(u - split, 4)
+                late = u - split - 4 * group
+                return jnp.where(u < split, u, jnp.where(late < 3, 3 * group + late, split + group))
+
             def step(u, _):
-                h = lax.div(u, n_gu)
-
-                @pl.when(u == n_gu - 1)
+                whole = (u >= split) & (lax.rem(u - split + 4, 4) == 3)
+
+                @pl.when(u == split - 1)
                 def _():
                     finish_sum(0, 0, 3, n_down)
 
-                @pl.when(u == n_gu)
+                @pl.when(u == split)
                 def _():
                     finish_wait(0, 0, 3, n_down)
                     norm_half(1)
 
-                gate_up(u, 2 * n_gu, h)
+                @pl.when(jnp.logical_not(whole))
+                def _():
+                    gate_up(u, steps, tile, jnp.where(u < split, 0, 1))
+
+                @pl.when(whole)
+                def _():
+                    gate_up(u, steps, tile, None)
+
                 return 0
 
-            lax.fori_loop(0, 2 * n_gu, step, 0)
+            lax.fori_loop(0, steps, step, 0)
 
         @pl.when(b == 1)
         def _():
@@ -367,7 +382,7 @@
                 def _():
                     chip_add(0, 1, n_down - 1)
 
-                gate_up(t, n_gu, None)
+                gate_up(t, n_gu, lambda u: u, None)
                 return 0
 
             lax.fori_loop(0, n_gu, step, 0)

time: 401 us -> 401 us (level)
  no operation moved by 1% of the time
where the time goes in v7:
time: 401 us
  Pallas kernels  388 us (97%)
  other arithmetic  6.26 us (2%)
  local copies, waits for them, and re-layouts  5.72 us (1%)
    pallas_call x1, Pallas kernels, shard_body(): pl.pallas_call(kernel, in_specs=[pl.BlockSpec(memory_space=pltpu.SMEM)] +...  388 us

profile of v7, /device:TPU:0, one launch (start us, length us, event | category | flops | bytes accessed | tf_op | source)
XLA Modules:
  0.0 400.5 jit_solution(3965464552838490386)
XLA Ops:
  0.6 387.9 %shard_map.148 = (bf16[512,3072]{1,0:T(8,128)(2,1)}, bf16[512,3072]{1,0:T(8,128)(2,1)}, bf16[2,2,4,512,256]{4,3,2,1,0:T(8,128)(2,1)}, bf16[2,2,4,512,256]{4,3,2,1,0:T(8,128)(2,1)}) custom-call(s32[2]{0:T(128)} %len_ref.1, bf16[2,512,3072]{2,1,0:T(8,128)(2,1)} %hidden.1, bf16[2,3072,4,256]{3,2,1,0:T(4,128)(2,1)} %w_query.1, bf16[2,3072,4,256]{3,2,1,0:T(4,128)(2,1)} %w_key.1, ...), custom_call_target="tpu_custom_call" | custom-call | tf_op jit(solution)/shard_map/pallas_call | solution.py:511
  388.5 0.0 copy-start.1
  388.5 6.3 %pad_maximum_fusion = bf16[2,512,3072]{2,1,0:T(8,128)(2,1)} fusion(bf16[1,512,3072]{2,1,0:T(8,128)(2,1)} %bitcast.5, bf16[1,512,3072]{2,1,0:T(8,128)(2,1)} %bitcast.4), kind=kLoop, calls=%fused_computation | loop fusion | flops 3145728 | bytes 12582912 | tf_op jit(solution)/shard_map/stack | solution.py:538
  394.8 0.0 copy-done.1
  394.8 0.0 copy-start
  394.8 2.1 copy.18
  396.9 1.6 copy-done
  398.5 2.0 copy.19
Async XLA Ops:
  388.5 6.3 %copy-start.1 = (bf16[2,2,4,512,256]{4,3,2,1,0:T(8,128)(2,1)S(1)}, bf16[2,2,4,512,256]{4,3,2,1,0:T(8,128)(2,1)}, u32[]{:S(2)}) copy-start(bf16[2,2,4,512,256]{4,3,2,1,0:T(8,128)(2,1)} %get-tuple-element.15) | copy-start | bytes 12582916
  394.8 3.7 copy-start
